TPU v7x, 32 devices: a whole 2x2x4 slice. The times are simulated.
32 devices in a mesh: dp: 2 (over x), seq: 16 (over z, y, core).
Axes of the slice: x: 2, y: 2, z: 4, core: 2. Of those that a mesh axis runs over, the one named last changes fastest.
Arguments:
- grad_out: bfloat16 [2, 4096, 512], P('dp', 'seq'), may hold values from -6 to 6
- gate: bfloat16 [2, 4096, 512], P('dp', 'seq'), may hold values from -6 to 6
- signal: bfloat16 [2, 4096, 512], P('dp', 'seq'), may hold values from -6 to 6
- filters: float32 [2, 256, 4096], P(None, 'seq', 'dp'), may hold values from -0.09375 to 0.09375
Outputs:
- grad_signal: bfloat16 [2, 4096, 512], P('dp', 'seq')
- grad_gate: bfloat16 [2, 4096, 512], P('dp', 'seq')
- grad_filter: float32 [2, 256, 4096], P(None, 'seq', 'dp')
All inputs are finite; a program needn't handle non-finite values.
Results may differ from a plain program's by a relative error of at most 0.005.
Values may be sent and summed in bfloat16 or wider, within the bound.
No kernel may reach another device: no remote copies, remote signals or barrier semaphores. Data moves between devices by JAX's collectives and lax.ppermute only.
A program may use at most 128 MiB of HBM per device.

v0:
```python
import functools

import jax
import jax.numpy as jnp
from jax import lax
from jax.experimental import pallas as pl
from jax.experimental.pallas import tpu as pltpu
from jax.sharding import PartitionSpec as P

LANES = 128
PACK = 16
AHEAD = 2
bf16 = jnp.bfloat16
f32 = jnp.float32


def iota(shape, axis):
    return lax.broadcasted_iota(jnp.int32, shape, axis)


def flip_matrix(size, dtype):
    hit = iota((size, size), 0) + iota((size, size), 1) == size - 1
    return jnp.where(hit, 1.0, 0.0).astype(dtype)


def times(a, b):
    return jnp.dot(a, b, preferred_element_type=f32)


def gather_rows(parts):
    return parts[0] if len(parts) == 1 else jnp.concatenate(parts, axis=0)


def send_kernel(sizes, out_grad, gate, signal, sent, grads, gates, signals, made, arrived, left):
    dp, seq, per, spd = sizes
    width = per * seq * spd
    pairs = ((signal, signals), (out_grad, grads), (gate, gates))
    coming = [
        [
            pltpu.make_async_copy(
                source.at[:, pl.ds(p * width, width)],
                held.at[:, pl.ds(p * width, width)],
                arrived.at[k, p],
            )
            for k, (source, held) in enumerate(pairs)
        ]
        for p in range(dp)
    ]
    going = [
        pltpu.make_async_copy(made.at[pl.ds(p * seq, seq)], sent.at[pl.ds(p * seq, seq)], left.at[p])
        for p in range(dp)
    ]
    for copies in coming:
        for copy in copies:
            copy.start()
    for p in range(dp):
        at = pl.ds(p * width, width)
        for copy in coming[p]:
            copy.wait()
        plain = signals[:, at].astype(f32).T
        scaled = (grads[:, at].astype(f32) * gates[:, at].astype(f32)).T
        for q in range(seq):
            parts = []
            for value in (scaled, plain):
                for s in range(spd):
                    begin = (s * seq + q) * per
                    parts.append(value[begin : begin + per])
            made[p * seq + q] = gather_rows(parts).astype(bf16)
        going[p].start()
    for copy in going:
        copy.wait()


def receive_kernel(sizes, got, out_grad, grad_signal, grad_gate):
    dp, seq, per, spd = sizes
    width = per * seq
    cpd = per * spd
    for p in range(dp):
        for s in range(spd):
            begin = (p * spd + s) * width
            turned = []
            for t in range(2):
                low = t * cpd + s * per
                block = got[p * seq : (p + 1) * seq].astype(f32)
                turned.append(gather_rows([block[q, low : low + per] for q in range(seq)]).T)
            grad = out_grad[:, begin : begin + width].astype(f32)
            grad_gate[:, begin : begin + width] = (grad * turned[0]).astype(bf16)
            grad_signal[:, begin : begin + width] = turned[1].astype(bf16)


def stage_flipped(dp, seq, cpd, got, held):
    tokens = got.shape[2]
    flip = flip_matrix(tokens, bf16)
    for b in range(dp):
        block = got[b * seq : (b + 1) * seq, :cpd].reshape(seq * cpd, tokens)
        turned = times(block, flip)
        for q in range(seq):
            to = pl.ds((b * seq + seq - 1 - q) * cpd, cpd)
            for half in range(tokens // LANES):
                held[half, to, :] = turned[q * cpd : (q + 1) * cpd, half * LANES : (half + 1) * LANES]


def skew(value):
    return pltpu.roll(value, 0, 1, stride=1, stride_axis=0)


def tile_kernel(taps, tiles):
    parts, cpd, per_part, _ = taps.shape
    lower = iota((LANES, LANES), 1) >= iota((LANES, LANES), 0)

    def channel(c, carry):
        before = jnp.zeros((LANES, LANES), f32)
        for d in range(parts * per_part):
            row = taps[d // per_part, c, pl.ds(d % per_part, 1), :]
            now = skew(jnp.broadcast_to(row, (LANES, LANES)))
            tiles[c, pl.ds(d * LANES, LANES), :] = jnp.where(lower, now, before).astype(bf16)
            before = now
        return carry

    lax.fori_loop(0, cpd, channel, 0)


def spread(line, shifted, u, streams, blocks):
    size = blocks * streams
    for k in range(PACK // streams):
        at = pl.ds(PACK - k * streams, size)
        shifted[u, k, size:] = line[u, at, :].astype(bf16)


def mix_kernel(sizes, got, taps, made, plain, turned, line, shifted, result, out):
    dp, seq, cpd = sizes
    tokens = got.shape[2]
    halves = tokens // LANES
    blocks = seq * halves
    streams = 2 * dp
    size = blocks * streams
    rows = dp * seq * cpd
    ahead = line.shape[0]
    value = got[:, cpd:].astype(f32).reshape(rows, tokens)
    for half in range(halves):
        plain[half] = value[:, half * LANES : (half + 1) * LANES]
    stage_flipped(dp, seq, cpd, got, turned)
    for u in range(ahead):
        line[u, :PACK] = jnp.zeros((PACK, LANES), f32)
        for k in range(PACK // streams):
            shifted[u, k, :size] = jnp.zeros((size, LANES), bf16)
    lower = iota((LANES, LANES), 1) >= iota((LANES, LANES), 0)
    held = (plain, turned)
    order = [(k, b, half) for k in range(2) for b in range(dp) for half in range(halves)]

    def channel(c, u):
        for kind, b, half in order:
            rows = pl.ds(b * seq * cpd + c, seq, stride=cpd)
            to = pl.ds(PACK + half * streams + kind * dp + b, seq, stride=halves * streams)
            line[u, to, :] = held[kind][half, rows, :]
        spread(line, shifted, u, streams, blocks)
        total = [None, None]
        before = jnp.zeros((LANES, LANES), f32)
        for e in range(blocks // 2):
            tiles = []
            for d in (2 * e, 2 * e + 1):
                row = taps[d // taps.shape[2], c, pl.ds(d % taps.shape[2], 1), :]
                now = skew(jnp.broadcast_to(row, (LANES, LANES)))
                tiles.append(jnp.where(lower, now, before).astype(bf16))
                before = now
            which = 0 if 4 * e < blocks else 1
            count = size >> which
            left = []
            for d in (2 * e, 2 * e + 1):
                k = d % (PACK // streams)
                at = 2 * size - count - (d - k) * streams
                left.append(shifted[u, k, pl.ds(at, count), :])
            product = times(jnp.concatenate(left, axis=1), jnp.concatenate(tiles, axis=0))
            total[which] = product if total[which] is None else total[which] + product
        result[u, : size // 2] = total[0][: size // 2]
        result[u, size // 2 :] = total[0][size // 2 :] + total[1]
        for kind, b, half in order:
            rows = pl.ds(b * seq * cpd + c, seq, stride=cpd)
            at = pl.ds(half * streams + kind * dp + b, seq, stride=halves * streams)
            out[kind, half, rows, :] = result[u, at, :]

    def step(i, carry):
        for u in range(ahead):
            channel(i * ahead + u, u)
        return carry

    lax.fori_loop(0, cpd // ahead, step, 0)
    flip = flip_matrix(tokens, bf16)
    for kind in range(2):
        for b in range(dp):
            at = pl.ds(b * seq * cpd, seq * cpd)
            value = jnp.concatenate([out[kind, half, at, :] for half in range(halves)], axis=1).astype(bf16)
            if kind == 1:
                value = times(value, flip).astype(bf16)
            for q in range(seq):
                to = b * seq + (q if kind == 0 else seq - 1 - q)
                made[to, kind * cpd : (kind + 1) * cpd] = value[q * cpd : (q + 1) * cpd]


def tap_kernel(sizes, factor, got, made, mirrored, turned, plain, line, shifted, square, partial, lags):
    dp, seq, cpd = sizes
    tokens = got.shape[2]
    halves = tokens // LANES
    blocks = seq * halves
    streams = 2 * dp
    size = blocks * streams
    small = LANES // 2
    ahead = line.shape[0]
    stage_flipped(dp, seq, cpd, got, turned)
    for b in range(dp):
        for q in range(seq):
            block = got[b * seq + q].astype(f32)[cpd:]
            to = pl.ds((b * seq + seq - 1 - q) * cpd, cpd)
            for half in range(halves):
                mirrored[halves - 1 - half, to, :] = block[:, half * LANES : (half + 1) * LANES]
    for u in range(ahead):
        line[u, :PACK] = jnp.zeros((PACK, LANES), f32)
        for b in range(dp):
            plain[u, b, :8] = jnp.zeros((8, LANES), f32)
        for k in range(PACK // streams):
            shifted[u, k, :size] = jnp.zeros((size, LANES), bf16)
    low_half = iota((blocks, LANES), 1) < small
    lower = iota((small, LANES), 1) >= iota((small, LANES), 0)

    def channel(c, u):
        for b in range(dp):
            for half in range(halves):
                rows = pl.ds(b * seq * cpd + c, seq, stride=cpd)
                plain[u, b, pl.ds(8 + half, seq, stride=halves), :] = turned[half, rows, :]
                value = mirrored[half, rows, :]
                for k in range(2):
                    to = pl.ds(half * streams + k * dp + b, seq, stride=halves * streams)
                    square[u, to, :] = pltpu.roll(value, small, 1) if k else value
        for b in range(dp):
            here = plain[u, b, 8:]
            behind = plain[u, b, pl.ds(7, blocks), :]
            late = jnp.where(low_half, pltpu.roll(behind, small, 1), pltpu.roll(here, small, 1))
            line[u, pl.ds(PACK + b, blocks, stride=streams), :] = here
            line[u, pl.ds(PACK + dp + b, blocks, stride=streams), :] = late
        spread(line, shifted, u, streams, blocks)
        left = square[u].T[:small].astype(bf16)
        before = jnp.zeros((small, LANES), f32)
        for pair in range(blocks // 2):
            right = []
            for at in (2 * pair + 1, 2 * pair + 2):
                k = -at % (PACK // streams)
                right.append(shifted[u, k, pl.ds((at + k) * streams, size), :])
            product = times(left, jnp.concatenate(right, axis=1))
            for k in range(2):
                now = skew(product[:, k * LANES : (k + 1) * LANES])
                value = jnp.where(lower, now, before)
                before = now
                value = jnp.sum(value.reshape(small // 8, 8, LANES), axis=0)
                partial[u, pl.ds((2 * pair + k) * 8, 8), :] = value
        total = partial[u, pl.ds(0, blocks, stride=8), :]
        for j in range(1, 8):
            total = total + partial[u, pl.ds(j, blocks, stride=8), :]
        lags[pl.ds(c * blocks, blocks), :] = total * factor

    def step(i, carry):
        for u in range(ahead):
            channel(i * ahead + u, u)
        return carry

    lax.fori_loop(0, cpd // ahead, step, 0)
    flip = flip_matrix(LANES, f32)
    lags[...] = jnp.dot(lags[...], flip, preferred_element_type=f32, precision=lax.Precision.HIGHEST)
    per_part = blocks // made.shape[0]
    for k in range(blocks):
        column = pl.ds((k % per_part) * LANES, LANES)
        made[k // per_part, :, column] = lags[pl.ds(blocks - 1 - k, cpd, stride=blocks), :]


def exchange(blocks, axis):
    size = blocks.shape[0]
    me = lax.axis_index(axis)
    own = lax.dynamic_index_in_dim(blocks, me, 0, True)
    result = lax.dynamic_update_slice_in_dim(jnp.zeros_like(blocks), own, me, 0)
    for k in range(1, size):
        part = lax.dynamic_index_in_dim(blocks, (me + k) % size, 0, True)
        part = lax.ppermute(part, axis, [(i, (i + k) % size) for i in range(size)])
        result = lax.dynamic_update_slice_in_dim(result, part, (me - k) % size, 0)
    return result


def call(kernel, out_shape, scratch=(), flops=0, limit=16, specs=None):
    extra = {} if specs is None else dict(in_specs=specs[0], out_specs=specs[1])
    return pl.pallas_call(
        kernel,
        out_shape=out_shape,
        scratch_shapes=list(scratch),
        cost_estimate=pl.CostEstimate(flops=flops, bytes_accessed=1 << 20, transcendentals=0),
        compiler_params=pltpu.CompilerParams(vmem_limit_bytes=limit << 20),
        **extra,
    )


def on_device(grad_out, gate, signal, filters):
    shape = jax.ShapeDtypeStruct
    dp, seq = lax.axis_size("dp"), lax.axis_size("seq")
    tokens, channels = grad_out.shape[1:]
    segments, per, part = filters.shape
    spd = segments // dp
    cpd = spd * per
    length = tokens * seq
    halves = tokens // LANES
    blocks = length // LANES
    rows = dp * seq * cpd
    streams = 2 * dp
    size = blocks * streams
    copies = PACK // streams
    ahead = AHEAD if cpd % AHEAD == 0 else 1
    both = ("dp", "seq")
    taps = exchange(filters.reshape(dp, cpd, part // LANES, LANES), "dp")
    edge = (dp, seq, per, spd)
    anywhere = pl.BlockSpec(memory_space=pl.ANY)
    sent = call(
        functools.partial(send_kernel, edge),
        shape((dp * seq, 2 * cpd, tokens), bf16),
        (
            pltpu.VMEM((tokens, channels), bf16),
            pltpu.VMEM((tokens, channels), bf16),
            pltpu.VMEM((tokens, channels), bf16),
            pltpu.VMEM((dp * seq, 2 * cpd, tokens), bf16),
            pltpu.SemaphoreType.DMA((3, dp)),
            pltpu.SemaphoreType.DMA((dp,)),
        ),
        limit=63,
        specs=([anywhere] * 3, anywhere),
    )(grad_out[0], gate[0], signal[0])
    got = lax.all_to_all(sent, both, split_axis=0, concat_axis=0, tiled=True)
    inner = (dp, seq, cpd)
    made = call(
        functools.partial(mix_kernel, inner),
        shape((dp * seq, 2 * cpd, tokens), bf16),
        (
            pltpu.VMEM((halves, rows, LANES), f32),
            pltpu.VMEM((halves, rows, LANES), f32),
            pltpu.VMEM((ahead, PACK + size, LANES), f32),
            pltpu.VMEM((ahead, copies, 2 * size, LANES), bf16),
            pltpu.VMEM((ahead, size, LANES), f32),
            pltpu.VMEM((2, halves, rows, LANES), f32),
        ),
    )(got, taps)
    back = lax.all_to_all(made, both, split_axis=0, concat_axis=0, tiled=True)
    lags = call(
        functools.partial(tap_kernel, inner, float(dp * length) ** -0.5),
        shape((dp, cpd, part), f32),
        (
            pltpu.VMEM((halves, rows, LANES), f32),
            pltpu.VMEM((halves, rows, LANES), f32),
            pltpu.VMEM((ahead, dp, 8 + blocks, LANES), f32),
            pltpu.VMEM((ahead, PACK + size, LANES), f32),
            pltpu.VMEM((ahead, copies, 2 * size, LANES), bf16),
            pltpu.VMEM((ahead, size, LANES), f32),
            pltpu.VMEM((ahead, blocks * 8, LANES), f32),
            pltpu.VMEM((cpd * blocks, LANES), f32),
        ),
        flops=1 << 30,
    )(got)
    grad_filter = exchange(lags, "dp").reshape(segments, per, part)
    grad_signal, grad_gate = call(
        functools.partial(receive_kernel, edge),
        (shape((tokens, channels), bf16), shape((tokens, channels), bf16)),
    )(back, grad_out[0])
    return (grad_signal[None], grad_gate[None], grad_filter)


def solution(mesh):
    tokens = P("dp", "seq", None)
    taps = P(None, "seq", "dp")
    return jax.shard_map(
        on_device,
        mesh=mesh,
        in_specs=(tokens, tokens, tokens, taps),
        out_specs=(tokens, tokens, taps),
        check_vma=False,
    )
```

profile of v0, /device:TPU:0, one launch (start us, length us, event | category | flops | bytes accessed | tf_op | source)
XLA Modules:
  0.0 54.0 jit_solution(10656888063828920983)
XLA Ops:
  0.6 2.1 %shard_map.67 = bf16[32,32,256]{2,1,0:T(8,128)(2,1)} custom-call(bf16[256,512]{1,0:T(8,128)(2,1)} %bitcast.9, bf16[256,512]{1,0:T(8,128)(2,1)} %bitcast.12, bf16[256,512]{1,0:T(8,128)(2,1)} %bitcast.13), custom_call_target="tpu_custom_call" | custom-call | bytes 1048576 | tf_op jit(solution)/shard_map/pallas_call | solution.py:317
  2.7 0.0 copy-start.1
  2.8 7.3 %all-to-all-start = ((bf16[32,32,256]{2,1,0:T(8,128)(2,1)}), bf16[32,32,256]{2,1,0:T(8,128)(2,1)S(1)}, u32[]{:S(2)}, u32[]{:S(2)}) async-start(bf16[32,32,256]{2,1,0:T(8,128)(2,1)} %shard_map.67), calls=%async_computation | async-start | bytes 1048576 | tf_op jit(solution)/shard_map/all_to_all | solution.py:331
  10.1 0.0 copy-done.1
  10.2 1.8 %collective-permute-start = (f32[1,16,16,128]{3,2,1,0:T(8,128)S(1)}, f32[1,16,16,128]{3,2,1,0:T(8,128)S(1)}, u32[]{:S(2)}, u32[]{:S(2)}) collective-permute-start(f32[1,16,16,128]{3,2,1,0:T(8,128)S(1)} %get-tuple-element.9), channel_id=1, source_target_pairs={{0,16},{16,0},{1,17},{17,1},{2,18},{18,2},{3,19},{19,3},{4,20},{20... | collective-permute-start | bytes 393224 | tf_op jit(solution)/shard_map/ppermute | solution.py:281
  12.1 7.6 %collective-permute-done = f32[1,16,16,128]{3,2,1,0:T(8,128)S(1)} collective-permute-done((f32[1,16,16,128]{3,2,1,0:T(8,128)S(1)}, f32[1,16,16,128]{3,2,1,0:T(8,128)S(1)}, u32[]{:S(2)}, u32[]{:S(2)}) %collective-permute-start) | collective-permute-done | bytes 131104 | tf_op jit(solution)/shard_map/ppermute | solution.py:281
  19.7 6.3 %all-to-all-done.got = bf16[32,32,256]{2,1,0:T(8,128)(2,1)S(1)} async-done(((bf16[32,32,256]{2,1,0:T(8,128)(2,1)}), bf16[32,32,256]{2,1,0:T(8,128)(2,1)S(1)}, u32[]{:S(2)}, u32[]{:S(2)}) %all-to-all-start) | async-done | bytes 524320 | tf_op jit(solution)/shard_map/all_to_all | solution.py:331
  26.0 8.5 %shard_map.68 = bf16[32,32,256]{2,1,0:T(8,128)(2,1)} custom-call(bf16[32,32,256]{2,1,0:T(8,128)(2,1)S(1)} %all-to-all-done.got, f32[2,16,16,128]{3,2,1,0:T(8,128)S(1)} %constant_dynamic-update-slice_fusion.1.taps), custom_call_target="tpu_custom_call" | custom-call | bytes 1048576 | tf_op jit(solution)/shard_map/pallas_call | solution.py:333
  34.5 2.6 %all-to-all-start.1 = ((bf16[32,32,256]{2,1,0:T(8,128)(2,1)}), bf16[32,32,256]{2,1,0:T(8,128)(2,1)S(1)}, u32[]{:S(2)}, u32[]{:S(2)}) async-start(bf16[32,32,256]{2,1,0:T(8,128)(2,1)} %shard_map.68), calls=%async_computation.1 | async-start | bytes 1048576 | tf_op jit(solution)/shard_map/all_to_all | solution.py:345
  37.1 9.0 %shard_map.70 = f32[2,16,2048]{2,1,0:T(8,128)S(1)} custom-call(bf16[32,32,256]{2,1,0:T(8,128)(2,1)S(1)} %all-to-all-done.got), custom_call_target="tpu_custom_call" | custom-call | flops 1073741824 | bytes 1048576 | tf_op jit(solution)/shard_map/pallas_call | solution.py:346
  46.2 0.0 copy-start
  46.2 1.7 %collective-permute-start.1 = (f32[1,16,2048]{2,1,0:T(8,128)S(1)}, f32[1,16,2048]{2,1,0:T(8,128)S(1)}, u32[]{:S(2)}, u32[]{:S(2)}) collective-permute-start(f32[1,16,2048]{2,1,0:T(8,128)S(1)} %get-tuple-element.7), channel_id=1, source_target_pairs={{0,16},{16,0},{1,17},{17,1},{2,18},{18,2},{3,19},{19,3},{4,20},{20... | collective-permute-start | bytes 393224 | tf_op jit(solution)/shard_map/ppermute | solution.py:281
  47.9 4.7 %collective-permute-done.1 = f32[1,16,2048]{2,1,0:T(8,128)S(1)} collective-permute-done((f32[1,16,2048]{2,1,0:T(8,128)S(1)}, f32[1,16,2048]{2,1,0:T(8,128)S(1)}, u32[]{:S(2)}, u32[]{:S(2)}) %collective-permute-start.1) | collective-permute-done | bytes 131104 | tf_op jit(solution)/shard_map/ppermute | solution.py:281
  52.6 0.0 copy-start.2
  52.7 0.3 all-to-all-done.1.got
  53.0 0.0 copy-done
  53.0 1.0 %shard_map.69 = (bf16[256,512]{1,0:T(8,128)(2,1)}, bf16[256,512]{1,0:T(8,128)(2,1)}) custom-call(bf16[32,32,256]{2,1,0:T(8,128)(2,1)S(1)} %all-to-all-done.1.got, bf16[256,512]{1,0:T(8,128)(2,1)S(1)} %bitcast.10), custom_call_target="tpu_custom_call" | custom-call | bytes 1048576 | tf_op jit(solution)/shard_map/pallas_call | solution.py:362
  54.0 0.0 copy-done.2
  (7 shorter events, 0.2 us)
Async XLA Ops:
  2.7 7.4 %copy-start.1 = (f32[2,16,2048]{2,1,0:T(8,128)S(1)}, f32[2,16,2048]{2,1,0:T(8,128)}, u32[]{:S(2)}) copy-start(f32[2,16,2048]{2,1,0:T(8,128)} %param.7) | copy-start | bytes 786436
  2.8 23.2 %all-to-all-start = ((bf16[32,32,256]{2,1,0:T(8,128)(2,1)}), bf16[32,32,256]{2,1,0:T(8,128)(2,1)S(1)}, u32[]{:S(2)}, u32[]{:S(2)}) async-start(bf16[32,32,256]{2,1,0:T(8,128)(2,1)} %shard_map.67), calls=%async_computation | async-start | bytes 1048576 | tf_op jit(solution)/shard_map/all_to_all | solution.py:331
  10.2 9.4 %collective-permute-start = (f32[1,16,16,128]{3,2,1,0:T(8,128)S(1)}, f32[1,16,16,128]{3,2,1,0:T(8,128)S(1)}, u32[]{:S(2)}, u32[]{:S(2)}) collective-permute-start(f32[1,16,16,128]{3,2,1,0:T(8,128)S(1)} %get-tuple-element.9), channel_id=1, source_target_pairs={{0,16},{16,0},{1,17},{17,1},{2,18},{18,2},{3,19},{19,3},{4,20},{20... | collective-permute-start | bytes 393224 | tf_op jit(solution)/shard_map/ppermute | solution.py:281
  34.5 18.5 %all-to-all-start.1 = ((bf16[32,32,256]{2,1,0:T(8,128)(2,1)}), bf16[32,32,256]{2,1,0:T(8,128)(2,1)S(1)}, u32[]{:S(2)}, u32[]{:S(2)}) async-start(bf16[32,32,256]{2,1,0:T(8,128)(2,1)} %shard_map.68), calls=%async_computation.1 | async-start | bytes 1048576 | tf_op jit(solution)/shard_map/all_to_all | solution.py:345
  46.2 6.8 %copy-start = (bf16[1,256,512]{2,1,0:T(8,128)(2,1)S(1)}, bf16[1,256,512]{2,1,0:T(8,128)(2,1)}, u32[]{:S(2)}) copy-start(bf16[1,256,512]{2,1,0:T(8,128)(2,1)} %param.4) | copy-start | bytes 786436
  46.2 6.4 %collective-permute-start.1 = (f32[1,16,2048]{2,1,0:T(8,128)S(1)}, f32[1,16,2048]{2,1,0:T(8,128)S(1)}, u32[]{:S(2)}, u32[]{:S(2)}) collective-permute-start(f32[1,16,2048]{2,1,0:T(8,128)S(1)} %get-tuple-element.7), channel_id=1, source_target_pairs={{0,16},{16,0},{1,17},{17,1},{2,18},{18,2},{3,19},{19,3},{4,20},{20... | collective-permute-start | bytes 393224 | tf_op jit(solution)/shard_map/ppermute | solution.py:281
  52.6 1.3 %copy-start.2 = (f32[2,16,2048]{2,1,0:T(8,128)}, f32[2,16,2048]{2,1,0:T(8,128)S(1)}, u32[]{:S(2)}) copy-start(f32[2,16,2048]{2,1,0:T(8,128)S(1)} %constant_dynamic-update-slice_fusion) | copy-start | bytes 786436
where the time goes:
time: 54.3 us; the launch traced here: 54 us
  Pallas kernels  20.6 us (38%)
  waiting for transfers between devices  18.9 us (35%)
  starting transfers between devices  13.5 us (25%)
  between operations  0.77 us (1%)
    ppermute x2, waiting for transfers between devices, exchange(): part = lax.ppermute(part, axis, [(i, (i + k) % size) for i in range(size)])  12.3 us
    pallas_call x1, Pallas kernels, on_device(): call(functools.partial(tap_kernel, inner, float(dp * length) ** (-0.5)),...  9.01 us
    pallas_call x1, Pallas kernels, on_device(): call(functools.partial(mix_kernel, inner), shape((dp * seq, 2 * cpd, toke...  8.53 us
    all_to_all x1, starting transfers between devices, on_device(): got = lax.all_to_all(sent, both, split_axis=0, concat_axis=0, tiled=True)  7.33 us
    all_to_all x1, waiting for transfers between devices, on_device(): got = lax.all_to_all(sent, both, split_axis=0, concat_axis=0, tiled=True)  6.26 us
    ppermute x2, starting transfers between devices, exchange(): part = lax.ppermute(part, axis, [(i, (i + k) % size) for i in range(size)])  3.54 us
    all_to_all x1, starting transfers between devices, on_device(): back = lax.all_to_all(made, both, split_axis=0, concat_axis=0, tiled=True)  2.6 us
    pallas_call x1, Pallas kernels, on_device(): call(functools.partial(send_kernel, edge), shape((dp * seq, 2 * cpd, toke...  2.1 us
  transfers between devices with their start and end apart: 4, of which 4 were waited for; matrix products, arithmetic and copies ran while one was open for 0% of the time, Pallas kernels for 17%

commit v1 on v0

v1 whole, which is shorter than its diff:
```python
import functools

import jax
import jax.numpy as jnp
from jax import lax
from jax.experimental import pallas as pl
from jax.experimental.pallas import tpu as pltpu
from jax.sharding import PartitionSpec as P

LANES = 128
PACK = 16
AHEAD = 2
bf16 = jnp.bfloat16
f32 = jnp.float32


def iota(shape, axis):
    return lax.broadcasted_iota(jnp.int32, shape, axis)


def flip_matrix(size, dtype):
    hit = iota((size, size), 0) + iota((size, size), 1) == size - 1
    return jnp.where(hit, 1.0, 0.0).astype(dtype)


def times(a, b):
    return jnp.dot(a, b, preferred_element_type=f32)


def gather_rows(parts):
    return parts[0] if len(parts) == 1 else jnp.concatenate(parts, axis=0)


def send_kernel(sizes, out_grad, gate, signal, sent, grads, gates, signals, made, arrived, left):
    dp, seq, per, spd = sizes
    width = per * seq * spd
    pairs = ((signal, signals), (out_grad, grads), (gate, gates))
    coming = [
        [
            pltpu.make_async_copy(
                source.at[:, pl.ds(p * width, width)],
                held.at[:, pl.ds(p * width, width)],
                arrived.at[k, p],
            )
            for k, (source, held) in enumerate(pairs)
        ]
        for p in range(dp)
    ]
    going = [
        pltpu.make_async_copy(made.at[pl.ds(p * seq, seq)], sent.at[pl.ds(p * seq, seq)], left.at[p])
        for p in range(dp)
    ]
    for copies in coming:
        for copy in copies:
            copy.start()
    for p in range(dp):
        at = pl.ds(p * width, width)
        for copy in coming[p]:
            copy.wait()
        plain = signals[:, at].astype(f32).T
        scaled = (grads[:, at].astype(f32) * gates[:, at].astype(f32)).T
        for q in range(seq):
            parts = []
            for value in (scaled, plain):
                for s in range(spd):
                    begin = (s * seq + q) * per
                    parts.append(value[begin : begin + per])
            made[p * seq + q] = gather_rows(parts).astype(bf16)
        going[p].start()
    for copy in going:
        copy.wait()


def receive_kernel(sizes, got, out_grad, grad_signal, grad_gate):
    dp, seq, per, spd = sizes
    width = per * seq
    cpd = per * spd
    for p in range(dp):
        for s in range(spd):
            begin = (p * spd + s) * width
            turned = []
            for t in range(2):
                low = t * cpd + s * per
                block = got[p * seq : (p + 1) * seq].astype(f32)
                turned.append(gather_rows([block[q, low : low + per] for q in range(seq)]).T)
            grad = out_grad[:, begin : begin + width].astype(f32)
            grad_gate[:, begin : begin + width] = (grad * turned[0]).astype(bf16)
            grad_signal[:, begin : begin + width] = turned[1].astype(bf16)


def slots(b, seq, pitch, first=1):
    return (b * (seq + 1) + first) * pitch


def clear_slots(dp, seq, pitch, held):
    for b in range(dp):
        for half in range(held.shape[0]):
            held[half, pl.ds(slots(b, seq, pitch, 0), pitch), :] = jnp.zeros((pitch, LANES), f32)


def put(held, half, at, value):
    held[half, pl.ds(at, value.shape[0]), :] = value[:, half * LANES : (half + 1) * LANES]


def stage_flipped(dp, seq, cpd, got, held):
    tokens = got.shape[2]
    flip = flip_matrix(tokens, bf16)
    for b in range(dp):
        block = got[b * seq : (b + 1) * seq, :cpd].reshape(seq * cpd, tokens)
        turned = times(block, flip)
        for q in range(seq):
            to = slots(b, seq, cpd + 1) + (seq - 1 - q) * (cpd + 1)
            for half in range(2):
                put(held, half, to, turned[q * cpd : (q + 1) * cpd])


def skew(value):
    return pltpu.roll(value, 0, 1, stride=1, stride_axis=0)


def mix_kernel(sizes, got, taps, made, plain, turned, line, shifted, result, out):
    dp, seq, cpd = sizes
    tokens = got.shape[2]
    streams = 2 * dp
    small = LANES // 2
    quarters = tokens // small
    group = quarters * streams
    size = seq * group
    pitch = cpd + 1
    ahead = line.shape[0]
    per_part = taps.shape[2]
    for b in range(dp):
        for q in range(seq):
            value = got[b * seq + q].astype(f32)[cpd:]
            for half in range(2):
                put(plain, half, slots(b, seq, pitch) + q * pitch, value)
    stage_flipped(dp, seq, cpd, got, turned)
    held = (plain, turned)
    for one in held:
        clear_slots(dp, seq, pitch, one)
    for u in range(ahead):
        shifted[u, :size] = jnp.zeros((size, LANES), bf16)
        result[u, 1, : 2 * streams + 1] = jnp.zeros((2 * streams + 1, LANES), f32)
    lower = iota((small, LANES), 1) >= iota((small, LANES), 0)
    low = iota((seq, LANES), 1) < small
    order = [(k, b, half) for k in range(2) for b in range(dp) for half in range(2)]

    def channel(c, u):
        for kind, b, half in order:
            stream = kind * dp + b
            here = held[kind][half, pl.ds(slots(b, seq, pitch) + c, seq, stride=pitch), :]
            behind = held[kind][half, pl.ds(slots(b, seq, pitch, 0) + c, seq, stride=pitch), :]
            crossed = pltpu.roll(jnp.where(low, behind, here), small, 1)
            to = 2 * half * streams + stream
            line[u, pl.ds(to, seq, stride=group + 1), :] = jnp.where(low, here, crossed)
            line[u, pl.ds(to + streams, seq, stride=group + 1), :] = jnp.where(low, crossed, behind)
        for q in range(seq):
            shifted[u, size + q * group : size + (q + 1) * group] = line[u, pl.ds(q * (group + 1), group), :].astype(bf16)
        before = jnp.zeros((small, LANES), bf16)
        sums = []
        for which in range(2):
            left, tiles = [], []
            count = size >> which
            for f in range(which * seq // 4, (which + 1) * seq // 4):
                left.append(shifted[u, pl.ds(2 * size - count - 2 * f * group, count), :])
                pieces = []
                for d in range(4 * f, 4 * f + 4):
                    row = taps[d // per_part, c, pl.ds(d % per_part, 1), :]
                    now = skew(jnp.broadcast_to(row, (small, LANES))).astype(bf16)
                    pieces.append(jnp.where(lower, now, before))
                    before = now
                tiles.append(jnp.concatenate(pieces[:2], axis=1))
                tiles.append(jnp.concatenate(pieces[2:], axis=1))
            sums.append(times(jnp.concatenate(left, axis=1), jnp.concatenate(tiles, axis=0)))
        total = jnp.concatenate([sums[0][: size // 2], sums[0][size // 2 :] + sums[1]], axis=0)
        rows = 2 * streams
        late = jnp.concatenate([jnp.zeros((rows, LANES), f32), total[: size - rows, LANES:]], axis=0)
        total = total[:, :LANES] + late
        for k in range(2 * seq):
            result[u, k % 2, pl.ds((k // 2 + 1) * (rows + 1), rows), :] = total[k * rows : (k + 1) * rows]
        for kind, b, half in order:
            stream = kind * dp + b
            first = rows + 1 + stream
            even = result[u, half, pl.ds(first, seq, stride=rows + 1), :]
            here = result[u, half, pl.ds(first + streams, seq, stride=rows + 1), :]
            at = first + streams if half else stream + streams
            behind = result[u, 1 - half, pl.ds(at, seq, stride=rows + 1), :]
            value = even + pltpu.roll(jnp.where(low, here, behind), small, 1)
            out[kind, half, pl.ds(b * seq * pitch + c, seq, stride=pitch), :] = value

    def step(i, carry):
        for u in range(ahead):
            channel(i * ahead + u, u)
        return carry

    lax.fori_loop(0, cpd // ahead, step, 0)
    flip = flip_matrix(tokens, bf16)
    for kind in (1, 0):
        for b in range(dp):
            values = []
            for q in range(seq):
                at = pl.ds((b * seq + q) * pitch, cpd)
                values.append(jnp.concatenate([out[kind, half, at, :] for half in range(2)], axis=1).astype(bf16))
            if kind == 1:
                value = times(jnp.concatenate(values, axis=0), flip).astype(bf16)
                values = [value[q * cpd : (q + 1) * cpd] for q in range(seq)]
            for q in range(seq):
                to = b * seq + (q if kind == 0 else seq - 1 - q)
                made[to, kind * cpd : (kind + 1) * cpd] = values[q]


def tap_kernel(sizes, factor, got, made, mirrored, turned, line, flat, shifted, square, partial, lags):
    dp, seq, cpd = sizes
    streams = 2 * dp
    blocks = 2 * seq
    rows = 2 * streams
    size = seq * rows
    small = LANES // 2
    pitch = cpd + 1
    ahead = line.shape[0]
    stage_flipped(dp, seq, cpd, got, turned)
    clear_slots(dp, seq, pitch, turned)
    for b in range(dp):
        for q in range(seq):
            block = got[b * seq + q].astype(f32)[cpd:]
            to = pl.ds(slots(b, seq, pitch) + (seq - 1 - q) * pitch, cpd)
            for half in range(2):
                mirrored[1 - half, to, :] = block[:, half * LANES : (half + 1) * LANES]
    for u in range(ahead):
        flat[u, :PACK] = jnp.zeros((PACK, LANES), f32)
        for k in range(PACK // streams):
            shifted[u, k, :size] = jnp.zeros((size, LANES), bf16)
    low = iota((seq, LANES), 1) < small
    lower = iota((small, LANES), 1) >= iota((small, LANES), 0)

    def channel(c, u):
        for b in range(dp):
            here = [turned[half, pl.ds(slots(b, seq, pitch) + c, seq, stride=pitch), :] for half in range(2)]
            behind = [turned[1, pl.ds(slots(b, seq, pitch, 0) + c, seq, stride=pitch), :], here[0]]
            for half in range(2):
                late = pltpu.roll(jnp.where(low, here[half], behind[half]), small, 1)
                line[u, pl.ds(half * streams + b, seq, stride=rows + 1), :] = here[half]
                line[u, pl.ds(half * streams + dp + b, seq, stride=rows + 1), :] = late
                value = mirrored[half, pl.ds(slots(b, seq, pitch) + c, seq, stride=pitch), :]
                square[u, pl.ds(half * streams + b, seq, stride=rows + 1), :] = value
                square[u, pl.ds(half * streams + dp + b, seq, stride=rows + 1), :] = pltpu.roll(value, small, 1)
        for q in range(seq):
            flat[u, PACK + q * rows : PACK + (q + 1) * rows] = line[u, pl.ds(q * (rows + 1), rows), :]
        for k in range(PACK // streams):
            shifted[u, k, size:] = flat[u, pl.ds(PACK - k * streams, size), :].astype(bf16)
        wide = jnp.concatenate([square[u, pl.ds(q * (rows + 1), rows), :] for q in range(seq)], axis=0)
        left = wide.T[:small].astype(bf16)
        before = jnp.zeros((small, LANES), f32)
        for pair in range(blocks // 2):
            right = []
            for at in (2 * pair + 1, 2 * pair + 2):
                k = -at % (PACK // streams)
                right.append(shifted[u, k, pl.ds((at + k) * streams, size), :])
            product = times(left, jnp.concatenate(right, axis=1))
            for k in range(2):
                now = skew(product[:, k * LANES : (k + 1) * LANES])
                value = jnp.where(lower, now, before)
                before = now
                value = jnp.sum(value.reshape(small // 8, 8, LANES), axis=0)
                partial[u, pl.ds((2 * pair + k) * 9, 8), :] = value
        total = partial[u, pl.ds(0, blocks, stride=9), :]
        for j in range(1, 8):
            total = total + partial[u, pl.ds(j, blocks, stride=9), :]
        lags[pl.ds(c * (blocks + 1), blocks), :] = total * factor

    def step(i, carry):
        for u in range(ahead):
            channel(i * ahead + u, u)
        return carry

    lax.fori_loop(0, cpd // ahead, step, 0)
    flip = flip_matrix(LANES, f32)
    for c in range(cpd):
        at = pl.ds(c * (blocks + 1), blocks)
        lags[at, :] = jnp.dot(lags[at, :], flip, preferred_element_type=f32, precision=lax.Precision.HIGHEST)
    per_part = blocks // made.shape[0]
    for k in range(blocks):
        column = pl.ds((k % per_part) * LANES, LANES)
        made[k // per_part, :, column] = lags[pl.ds(blocks - 1 - k, cpd, stride=blocks + 1), :]


def exchange(blocks, axis):
    size = blocks.shape[0]
    me = lax.axis_index(axis)
    own = lax.dynamic_index_in_dim(blocks, me, 0, True)
    result = lax.dynamic_update_slice_in_dim(jnp.zeros_like(blocks), own, me, 0)
    for k in range(1, size):
        part = lax.dynamic_index_in_dim(blocks, (me + k) % size, 0, True)
        part = lax.ppermute(part, axis, [(i, (i + k) % size) for i in range(size)])
        result = lax.dynamic_update_slice_in_dim(result, part, (me - k) % size, 0)
    return result


def call(kernel, out_shape, scratch=(), flops=0, limit=16, specs=None):
    extra = {} if specs is None else dict(in_specs=specs[0], out_specs=specs[1])
    return pl.pallas_call(
        kernel,
        out_shape=out_shape,
        scratch_shapes=list(scratch),
        cost_estimate=pl.CostEstimate(flops=flops, bytes_accessed=1 << 20, transcendentals=0),
        compiler_params=pltpu.CompilerParams(vmem_limit_bytes=limit << 20),
        **extra,
    )


def on_device(grad_out, gate, signal, filters):
    shape = jax.ShapeDtypeStruct
    dp, seq = lax.axis_size("dp"), lax.axis_size("seq")
    tokens, channels = grad_out.shape[1:]
    segments, per, part = filters.shape
    spd = segments // dp
    cpd = spd * per
    length = tokens * seq
    blocks = length // LANES
    streams = 2 * dp
    group = 4 * streams
    slot_rows = dp * (seq + 1) * (cpd + 1)
    line_rows = seq * (2 * streams + 1)
    ahead = AHEAD if cpd % AHEAD == 0 else 1
    both = ("dp", "seq")
    taps = exchange(filters.reshape(dp, cpd, part // LANES, LANES), "dp")
    edge = (dp, seq, per, spd)
    anywhere = pl.BlockSpec(memory_space=pl.ANY)
    sent = call(
        functools.partial(send_kernel, edge),
        shape((dp * seq, 2 * cpd, tokens), bf16),
        (
            pltpu.VMEM((tokens, channels), bf16),
            pltpu.VMEM((tokens, channels), bf16),
            pltpu.VMEM((tokens, channels), bf16),
            pltpu.VMEM((dp * seq, 2 * cpd, tokens), bf16),
            pltpu.SemaphoreType.DMA((3, dp)),
            pltpu.SemaphoreType.DMA((dp,)),
        ),
        limit=63,
        specs=([anywhere] * 3, anywhere),
    )(grad_out[0], gate[0], signal[0])
    got = lax.all_to_all(sent, both, split_axis=0, concat_axis=0, tiled=True)
    inner = (dp, seq, cpd)
    made = call(
        functools.partial(mix_kernel, inner),
        shape((dp * seq, 2 * cpd, tokens), bf16),
        (
            pltpu.VMEM((2, slot_rows, LANES), f32),
            pltpu.VMEM((2, slot_rows, LANES), f32),
            pltpu.VMEM((ahead, seq * (group + 1), LANES), f32),
            pltpu.VMEM((ahead, 2 * seq * group, LANES), bf16),
            pltpu.VMEM((ahead, 2, line_rows + 2 * streams + 1, LANES), f32),
            pltpu.VMEM((2, 2, dp * seq * (cpd + 1), LANES), f32),
        ),
    )(got, taps)
    back = lax.all_to_all(made, both, split_axis=0, concat_axis=0, tiled=True)
    lags = call(
        functools.partial(tap_kernel, inner, float(dp * length) ** -0.5),
        shape((dp, cpd, part), f32),
        (
            pltpu.VMEM((2, slot_rows, LANES), f32),
            pltpu.VMEM((2, slot_rows, LANES), f32),
            pltpu.VMEM((ahead, line_rows, LANES), f32),
            pltpu.VMEM((ahead, PACK + blocks * streams, LANES), f32),
            pltpu.VMEM((ahead, PACK // streams, 2 * blocks * streams, LANES), bf16),
            pltpu.VMEM((ahead, line_rows, LANES), f32),
            pltpu.VMEM((ahead, blocks * 9, LANES), f32),
            pltpu.VMEM((cpd * (blocks + 1), LANES), f32),
        ),
        flops=1 << 30,
    )(got)
    grad_filter = exchange(lags, "dp").reshape(segments, per, part)
    grad_signal, grad_gate = call(
        functools.partial(receive_kernel, edge),
        (shape((tokens, channels), bf16), shape((tokens, channels), bf16)),
    )(back, grad_out[0])
    return (grad_signal[None], grad_gate[None], grad_filter)


def solution(mesh):
    tokens = P("dp", "seq", None)
    taps = P(None, "seq", "dp")
    return jax.shard_map(
        on_device,
        mesh=mesh,
        in_specs=(tokens, tokens, tokens, taps),
        out_specs=(tokens, tokens, taps),
        check_vma=False,
    )
```

time: 54.3 us -> 52.3 us (0.963)
  Pallas kernels: 20.6 us -> 18.6 us
    pallas_call x1, Pallas kernels: 8.53 us -> 6.53 us  [on_device(): call(functools.partial(mix_kernel, inner), shape((dp * seq, 2 * cpd, toke...]
where the time goes in v1:
time: 52.3 us; the launch traced here: 52 us
  waiting for transfers between devices  18.9 us (36%)
  Pallas kernels  18.6 us (36%)
  starting transfers between devices  13.5 us (26%)
  between operations  0.77 us (1%)
    ppermute x2, waiting for transfers between devices, exchange(): part = lax.ppermute(part, axis, [(i, (i + k) % size) for i in range(size)])  12.3 us
    pallas_call x1, Pallas kernels, on_device(): call(functools.partial(tap_kernel, inner, float(dp * length) ** (-0.5)),...  8.96 us
    all_to_all x1, starting transfers between devices, on_device(): got = lax.all_to_all(sent, both, split_axis=0, concat_axis=0, tiled=True)  7.33 us
    pallas_call x1, Pallas kernels, on_device(): call(functools.partial(mix_kernel, inner), shape((dp * seq, 2 * cpd, toke...  6.53 us
    all_to_all x1, waiting for transfers between devices, on_device(): got = lax.all_to_all(sent, both, split_axis=0, concat_axis=0, tiled=True)  6.26 us
    ppermute x2, starting transfers between devices, exchange(): part = lax.ppermute(part, axis, [(i, (i + k) % size) for i in range(size)])  3.56 us
    all_to_all x1, starting transfers between devices, on_device(): back = lax.all_to_all(made, both, split_axis=0, concat_axis=0, tiled=True)  2.6 us
    pallas_call x1, Pallas kernels, on_device(): call(functools.partial(send_kernel, edge), shape((dp * seq, 2 * cpd, toke...  2.1 us
  transfers between devices with their start and end apart: 4, of which 4 were waited for; matrix products, arithmetic and copies ran while one was open for 0% of the time, Pallas kernels for 17%

profile of v1, /device:TPU:0, one launch (start us, length us, event | category | flops | bytes accessed | tf_op | source)
XLA Modules:
  0.0 52.0 jit_solution(13023564413146779039)
XLA Ops:
  0.6 2.1 %shard_map.67 = bf16[32,32,256]{2,1,0:T(8,128)(2,1)} custom-call(bf16[256,512]{1,0:T(8,128)(2,1)} %bitcast.9, bf16[256,512]{1,0:T(8,128)(2,1)} %bitcast.12, bf16[256,512]{1,0:T(8,128)(2,1)} %bitcast.13), custom_call_target="tpu_custom_call" | custom-call | bytes 1048576 | tf_op jit(solution)/shard_map/pallas_call | solution.py:329
  2.7 0.0 copy-start.1
  2.8 7.3 %all-to-all-start = ((bf16[32,32,256]{2,1,0:T(8,128)(2,1)}), bf16[32,32,256]{2,1,0:T(8,128)(2,1)S(1)}, u32[]{:S(2)}, u32[]{:S(2)}) async-start(bf16[32,32,256]{2,1,0:T(8,128)(2,1)} %shard_map.67), calls=%async_computation | async-start | bytes 1048576 | tf_op jit(solution)/shard_map/all_to_all | solution.py:343
  10.1 0.0 copy-done.1
  10.2 1.8 %collective-permute-start = (f32[1,16,16,128]{3,2,1,0:T(8,128)S(1)}, f32[1,16,16,128]{3,2,1,0:T(8,128)S(1)}, u32[]{:S(2)}, u32[]{:S(2)}) collective-permute-start(f32[1,16,16,128]{3,2,1,0:T(8,128)S(1)} %get-tuple-element.9), channel_id=1, source_target_pairs={{0,16},{16,0},{1,17},{17,1},{2,18},{18,2},{3,19},{19,3},{4,20},{20... | collective-permute-start | bytes 393224 | tf_op jit(solution)/shard_map/ppermute | solution.py:294
  12.1 7.6 %collective-permute-done = f32[1,16,16,128]{3,2,1,0:T(8,128)S(1)} collective-permute-done((f32[1,16,16,128]{3,2,1,0:T(8,128)S(1)}, f32[1,16,16,128]{3,2,1,0:T(8,128)S(1)}, u32[]{:S(2)}, u32[]{:S(2)}) %collective-permute-start) | collective-permute-done | bytes 131104 | tf_op jit(solution)/shard_map/ppermute | solution.py:294
  19.7 6.3 %all-to-all-done.got = bf16[32,32,256]{2,1,0:T(8,128)(2,1)S(1)} async-done(((bf16[32,32,256]{2,1,0:T(8,128)(2,1)}), bf16[32,32,256]{2,1,0:T(8,128)(2,1)S(1)}, u32[]{:S(2)}, u32[]{:S(2)}) %all-to-all-start) | async-done | bytes 524320 | tf_op jit(solution)/shard_map/all_to_all | solution.py:343
  26.0 6.5 %shard_map.68 = bf16[32,32,256]{2,1,0:T(8,128)(2,1)} custom-call(bf16[32,32,256]{2,1,0:T(8,128)(2,1)S(1)} %all-to-all-done.got, f32[2,16,16,128]{3,2,1,0:T(8,128)S(1)} %constant_dynamic-update-slice_fusion.1.taps), custom_call_target="tpu_custom_call" | custom-call | bytes 1048576 | tf_op jit(solution)/shard_map/pallas_call | solution.py:345
  32.5 2.6 %all-to-all-start.1 = ((bf16[32,32,256]{2,1,0:T(8,128)(2,1)}), bf16[32,32,256]{2,1,0:T(8,128)(2,1)S(1)}, u32[]{:S(2)}, u32[]{:S(2)}) async-start(bf16[32,32,256]{2,1,0:T(8,128)(2,1)} %shard_map.68), calls=%async_computation.1 | async-start | bytes 1048576 | tf_op jit(solution)/shard_map/all_to_all | solution.py:357
  35.1 9.0 %shard_map.70 = f32[2,16,2048]{2,1,0:T(8,128)S(1)} custom-call(bf16[32,32,256]{2,1,0:T(8,128)(2,1)S(1)} %all-to-all-done.got), custom_call_target="tpu_custom_call" | custom-call | flops 1073741824 | bytes 1048576 | tf_op jit(solution)/shard_map/pallas_call | solution.py:358
  44.1 0.0 copy-start
  44.2 1.7 %collective-permute-start.1 = (f32[1,16,2048]{2,1,0:T(8,128)S(1)}, f32[1,16,2048]{2,1,0:T(8,128)S(1)}, u32[]{:S(2)}, u32[]{:S(2)}) collective-permute-start(f32[1,16,2048]{2,1,0:T(8,128)S(1)} %get-tuple-element.7), channel_id=1, source_target_pairs={{0,16},{16,0},{1,17},{17,1},{2,18},{18,2},{3,19},{19,3},{4,20},{20... | collective-permute-start | bytes 393224 | tf_op jit(solution)/shard_map/ppermute | solution.py:294
  45.9 4.7 %collective-permute-done.1 = f32[1,16,2048]{2,1,0:T(8,128)S(1)} collective-permute-done((f32[1,16,2048]{2,1,0:T(8,128)S(1)}, f32[1,16,2048]{2,1,0:T(8,128)S(1)}, u32[]{:S(2)}, u32[]{:S(2)}) %collective-permute-start.1) | collective-permute-done | bytes 131104 | tf_op jit(solution)/shard_map/ppermute | solution.py:294
  50.6 0.0 copy-start.2
  50.6 0.3 all-to-all-done.1.got
  51.0 0.0 copy-done
  51.0 1.0 %shard_map.69 = (bf16[256,512]{1,0:T(8,128)(2,1)}, bf16[256,512]{1,0:T(8,128)(2,1)}) custom-call(bf16[32,32,256]{2,1,0:T(8,128)(2,1)S(1)} %all-to-all-done.1.got, bf16[256,512]{1,0:T(8,128)(2,1)S(1)} %bitcast.10), custom_call_target="tpu_custom_call" | custom-call | bytes 1048576 | tf_op jit(solution)/shard_map/pallas_call | solution.py:374
  52.0 0.0 copy-done.2
  (7 shorter events, 0.2 us)
Async XLA Ops:
  2.7 7.4 %copy-start.1 = (f32[2,16,2048]{2,1,0:T(8,128)S(1)}, f32[2,16,2048]{2,1,0:T(8,128)}, u32[]{:S(2)}) copy-start(f32[2,16,2048]{2,1,0:T(8,128)} %param.7) | copy-start | bytes 786436
  2.8 23.2 %all-to-all-start = ((bf16[32,32,256]{2,1,0:T(8,128)(2,1)}), bf16[32,32,256]{2,1,0:T(8,128)(2,1)S(1)}, u32[]{:S(2)}, u32[]{:S(2)}) async-start(bf16[32,32,256]{2,1,0:T(8,128)(2,1)} %shard_map.67), calls=%async_computation | async-start | bytes 1048576 | tf_op jit(solution)/shard_map/all_to_all | solution.py:343
  10.2 9.4 %collective-permute-start = (f32[1,16,16,128]{3,2,1,0:T(8,128)S(1)}, f32[1,16,16,128]{3,2,1,0:T(8,128)S(1)}, u32[]{:S(2)}, u32[]{:S(2)}) collective-permute-start(f32[1,16,16,128]{3,2,1,0:T(8,128)S(1)} %get-tuple-element.9), channel_id=1, source_target_pairs={{0,16},{16,0},{1,17},{17,1},{2,18},{18,2},{3,19},{19,3},{4,20},{20... | collective-permute-start | bytes 393224 | tf_op jit(solution)/shard_map/ppermute | solution.py:294
  32.5 18.5 %all-to-all-start.1 = ((bf16[32,32,256]{2,1,0:T(8,128)(2,1)}), bf16[32,32,256]{2,1,0:T(8,128)(2,1)S(1)}, u32[]{:S(2)}, u32[]{:S(2)}) async-start(bf16[32,32,256]{2,1,0:T(8,128)(2,1)} %shard_map.68), calls=%async_computation.1 | async-start | bytes 1048576 | tf_op jit(solution)/shard_map/all_to_all | solution.py:357
  44.1 6.8 %copy-start = (bf16[1,256,512]{2,1,0:T(8,128)(2,1)S(1)}, bf16[1,256,512]{2,1,0:T(8,128)(2,1)}, u32[]{:S(2)}) copy-start(bf16[1,256,512]{2,1,0:T(8,128)(2,1)} %param.4) | copy-start | bytes 786436
  44.2 6.5 %collective-permute-start.1 = (f32[1,16,2048]{2,1,0:T(8,128)S(1)}, f32[1,16,2048]{2,1,0:T(8,128)S(1)}, u32[]{:S(2)}, u32[]{:S(2)}) collective-permute-start(f32[1,16,2048]{2,1,0:T(8,128)S(1)} %get-tuple-element.7), channel_id=1, source_target_pairs={{0,16},{16,0},{1,17},{17,1},{2,18},{18,2},{3,19},{19,3},{4,20},{20... | collective-permute-start | bytes 393224 | tf_op jit(solution)/shard_map/ppermute | solution.py:294
  50.6 1.3 %copy-start.2 = (f32[2,16,2048]{2,1,0:T(8,128)}, f32[2,16,2048]{2,1,0:T(8,128)S(1)}, u32[]{:S(2)}) copy-start(f32[2,16,2048]{2,1,0:T(8,128)S(1)} %constant_dynamic-update-slice_fusion) | copy-start | bytes 786436

commit v2 on v1

--- a/solution.py
+++ b/solution.py
@@ -53,12 +53,14 @@
     for copies in coming:
         for copy in copies:
             copy.start()
+    flip = flip_matrix(grads.shape[0], bf16)
     for p in range(dp):
         at = pl.ds(p * width, width)
         for copy in coming[p]:
             copy.wait()
+        scaled = (grads[:, at].astype(f32) * gates[:, at].astype(f32)).T
+        scaled = times(scaled.astype(bf16), flip)
         plain = signals[:, at].astype(f32).T
-        scaled = (grads[:, at].astype(f32) * gates[:, at].astype(f32)).T
         for q in range(seq):
             parts = []
             for value in (scaled, plain):
@@ -75,6 +77,7 @@
     dp, seq, per, spd = sizes
     width = per * seq
     cpd = per * spd
+    flip = flip_matrix(got.shape[2], bf16)
     for p in range(dp):
         for s in range(spd):
             begin = (p * spd + s) * width
@@ -82,7 +85,8 @@
             for t in range(2):
                 low = t * cpd + s * per
                 block = got[p * seq : (p + 1) * seq].astype(f32)
-                turned.append(gather_rows([block[q, low : low + per] for q in range(seq)]).T)
+                block = gather_rows([block[q, low : low + per] for q in range(seq)])
+                turned.append((times(block.astype(bf16), flip) if t else block).T)
             grad = out_grad[:, begin : begin + width].astype(f32)
             grad_gate[:, begin : begin + width] = (grad * turned[0]).astype(bf16)
             grad_signal[:, begin : begin + width] = turned[1].astype(bf16)
@@ -102,23 +106,21 @@
     held[half, pl.ds(at, value.shape[0]), :] = value[:, half * LANES : (half + 1) * LANES]
 
 
-def stage_flipped(dp, seq, cpd, got, held):
-    tokens = got.shape[2]
-    flip = flip_matrix(tokens, bf16)
+def stage(dp, seq, cpd, got, plain, turned):
+    pitch = cpd + 1
     for b in range(dp):
-        block = got[b * seq : (b + 1) * seq, :cpd].reshape(seq * cpd, tokens)
-        turned = times(block, flip)
-        for q in range(seq):
-            to = slots(b, seq, cpd + 1) + (seq - 1 - q) * (cpd + 1)
+        for q in range(seq):
+            value = got[b * seq + q].astype(f32)
             for half in range(2):
-                put(held, half, to, turned[q * cpd : (q + 1) * cpd])
+                put(plain, half, slots(b, seq, pitch) + q * pitch, value[cpd:])
+                put(turned, half, slots(b, seq, pitch) + (seq - 1 - q) * pitch, value[:cpd])
 
 
 def skew(value):
     return pltpu.roll(value, 0, 1, stride=1, stride_axis=0)
 
 
-def mix_kernel(sizes, got, taps, made, plain, turned, line, shifted, result, out):
+def mix_kernel(sizes, got, taps, made, plain, turned, line, shifted, result, out, done, left):
     dp, seq, cpd = sizes
     tokens = got.shape[2]
     streams = 2 * dp
@@ -128,14 +130,10 @@
     size = seq * group
     pitch = cpd + 1
     ahead = line.shape[0]
+
     per_part = taps.shape[2]
-    for b in range(dp):
-        for q in range(seq):
-            value = got[b * seq + q].astype(f32)[cpd:]
-            for half in range(2):
-                put(plain, half, slots(b, seq, pitch) + q * pitch, value)
-    stage_flipped(dp, seq, cpd, got, turned)
     held = (plain, turned)
+    stage(dp, seq, cpd, got, plain, turned)
     for one in held:
         clear_slots(dp, seq, pitch, one)
     for u in range(ahead):
@@ -159,10 +157,10 @@
         before = jnp.zeros((small, LANES), bf16)
         sums = []
         for which in range(2):
-            left, tiles = [], []
+            blocks, tiles = [], []
             count = size >> which
             for f in range(which * seq // 4, (which + 1) * seq // 4):
-                left.append(shifted[u, pl.ds(2 * size - count - 2 * f * group, count), :])
+                blocks.append(shifted[u, pl.ds(2 * size - count - 2 * f * group, count), :])
                 pieces = []
                 for d in range(4 * f, 4 * f + 4):
                     row = taps[d // per_part, c, pl.ds(d % per_part, 1), :]
@@ -171,7 +169,7 @@
                     before = now
                 tiles.append(jnp.concatenate(pieces[:2], axis=1))
                 tiles.append(jnp.concatenate(pieces[2:], axis=1))
-            sums.append(times(jnp.concatenate(left, axis=1), jnp.concatenate(tiles, axis=0)))
+            sums.append(times(jnp.concatenate(blocks, axis=1), jnp.concatenate(tiles, axis=0)))
         total = jnp.concatenate([sums[0][: size // 2], sums[0][size // 2 :] + sums[1]], axis=0)
         rows = 2 * streams
         late = jnp.concatenate([jnp.zeros((rows, LANES), f32), total[: size - rows, LANES:]], axis=0)
@@ -188,25 +186,28 @@
             value = even + pltpu.roll(jnp.where(low, here, behind), small, 1)
             out[kind, half, pl.ds(b * seq * pitch + c, seq, stride=pitch), :] = value
 
-    def step(i, carry):
-        for u in range(ahead):
-            channel(i * ahead + u, u)
-        return carry
-
-    lax.fori_loop(0, cpd // ahead, step, 0)
-    flip = flip_matrix(tokens, bf16)
-    for kind in (1, 0):
-        for b in range(dp):
-            values = []
-            for q in range(seq):
-                at = pl.ds((b * seq + q) * pitch, cpd)
-                values.append(jnp.concatenate([out[kind, half, at, :] for half in range(2)], axis=1).astype(bf16))
-            if kind == 1:
-                value = times(jnp.concatenate(values, axis=0), flip).astype(bf16)
-                values = [value[q * cpd : (q + 1) * cpd] for q in range(seq)]
-            for q in range(seq):
-                to = b * seq + (q if kind == 0 else seq - 1 - q)
-                made[to, kind * cpd : (kind + 1) * cpd] = values[q]
+    parts = left.shape[0]
+    each = cpd // parts
+    going = []
+    for part in range(parts):
+
+        def step(i, carry):
+            for u in range(ahead):
+                channel(part * each + i * ahead + u, u)
+            return carry
+
+        lax.fori_loop(0, each // ahead, step, 0)
+        for kind in range(2):
+            to = pl.ds(kind * cpd + part * each, each)
+            for b in range(dp):
+                for q in range(seq):
+                    at = pl.ds((b * seq + q) * pitch + part * each, each)
+                    value = jnp.concatenate([out[kind, half, at, :] for half in range(2)], axis=1)
+                    done[b * seq + (seq - 1 - q if kind else q), to, :] = value.astype(bf16)
+            going.append(pltpu.make_async_copy(done.at[:, to, :], made.at[:, to, :], left.at[part, kind]))
+            going[-1].start()
+    for copy in going:
+        copy.wait()
 
 
 def tap_kernel(sizes, factor, got, made, mirrored, turned, line, flat, shifted, square, partial, lags):
@@ -218,14 +219,15 @@
     small = LANES // 2
     pitch = cpd + 1
     ahead = line.shape[0]
-    stage_flipped(dp, seq, cpd, got, turned)
     clear_slots(dp, seq, pitch, turned)
     for b in range(dp):
         for q in range(seq):
-            block = got[b * seq + q].astype(f32)[cpd:]
-            to = pl.ds(slots(b, seq, pitch) + (seq - 1 - q) * pitch, cpd)
+            value = got[b * seq + q].astype(f32)
+            to = slots(b, seq, pitch) + (seq - 1 - q) * pitch
             for half in range(2):
-                mirrored[1 - half, to, :] = block[:, half * LANES : (half + 1) * LANES]
+                put(turned, half, to, value[:cpd])
+                at = pl.ds(to, cpd)
+                mirrored[1 - half, at, :] = value[cpd:, half * LANES : (half + 1) * LANES]
     for u in range(ahead):
         flat[u, :PACK] = jnp.zeros((PACK, LANES), f32)
         for k in range(PACK // streams):
@@ -322,6 +324,7 @@
     slot_rows = dp * (seq + 1) * (cpd + 1)
     line_rows = seq * (2 * streams + 1)
     ahead = AHEAD if cpd % AHEAD == 0 else 1
+    many = 4 if cpd % 16 == 0 else ahead
     both = ("dp", "seq")
     taps = exchange(filters.reshape(dp, cpd, part // LANES, LANES), "dp")
     edge = (dp, seq, per, spd)
@@ -342,17 +345,21 @@
     )(grad_out[0], gate[0], signal[0])
     got = lax.all_to_all(sent, both, split_axis=0, concat_axis=0, tiled=True)
     inner = (dp, seq, cpd)
+    parts = 2 if cpd % 16 == 0 else 1
     made = call(
         functools.partial(mix_kernel, inner),
         shape((dp * seq, 2 * cpd, tokens), bf16),
         (
             pltpu.VMEM((2, slot_rows, LANES), f32),
             pltpu.VMEM((2, slot_rows, LANES), f32),
-            pltpu.VMEM((ahead, seq * (group + 1), LANES), f32),
-            pltpu.VMEM((ahead, 2 * seq * group, LANES), bf16),
-            pltpu.VMEM((ahead, 2, line_rows + 2 * streams + 1, LANES), f32),
+            pltpu.VMEM((many, seq * (group + 1), LANES), f32),
+            pltpu.VMEM((many, 2 * seq * group, LANES), bf16),
+            pltpu.VMEM((many, 2, line_rows + 2 * streams + 1, LANES), f32),
             pltpu.VMEM((2, 2, dp * seq * (cpd + 1), LANES), f32),
+            pltpu.VMEM((dp * seq, 2 * cpd, tokens), bf16),
+            pltpu.SemaphoreType.DMA((parts, 2)),
         ),
+        specs=([pl.BlockSpec(memory_space=pltpu.VMEM)] * 2, anywhere),
     )(got, taps)
     back = lax.all_to_all(made, both, split_axis=0, concat_axis=0, tiled=True)
     lags = call(

time: 52.3 us -> 51.9 us (level)
  Pallas kernels: 18.6 us -> 17.9 us
    pallas_call x1, Pallas kernels: 6.53 us -> 5.74 us  [on_device(): call(functools.partial(mix_kernel, inner), shape((dp * seq, 2 * cpd, toke...]
where the time goes in v2:
time: 51.9 us; the launch traced here: 51.5 us
  waiting for transfers between devices  19.2 us (37%)
  Pallas kernels  17.9 us (34%)
  starting transfers between devices  13.5 us (26%)
  between operations  0.77 us (1%)
    ppermute x2, waiting for transfers between devices, exchange(): part = lax.ppermute(part, axis, [(i, (i + k) % size) for i in range(size)])  12.4 us
    pallas_call x1, Pallas kernels, on_device(): call(functools.partial(tap_kernel, inner, float(dp * length) ** (-0.5)),...  8.74 us
    all_to_all x1, starting transfers between devices, on_device(): got = lax.all_to_all(sent, both, split_axis=0, concat_axis=0, tiled=True)  7.33 us
    all_to_all x1, waiting for transfers between devices, on_device(): got = lax.all_to_all(sent, both, split_axis=0, concat_axis=0, tiled=True)  6.26 us
    pallas_call x1, Pallas kernels, on_device(): call(functools.partial(mix_kernel, inner), shape((dp * seq, 2 * cpd, toke...  5.74 us
    ppermute x2, starting transfers between devices, exchange(): part = lax.ppermute(part, axis, [(i, (i + k) % size) for i in range(size)])  3.54 us
    all_to_all x1, starting transfers between devices, on_device(): back = lax.all_to_all(made, both, split_axis=0, concat_axis=0, tiled=True)  2.62 us
    pallas_call x1, Pallas kernels, on_device(): call(functools.partial(send_kernel, edge), shape((dp * seq, 2 * cpd, toke...  2.32 us
  transfers between devices with their start and end apart: 4, of which 4 were waited for; matrix products, arithmetic and copies ran while one was open for 0% of the time, Pallas kernels for 17%

profile of v2, /device:TPU:0, one launch (start us, length us, event | category | flops | bytes accessed | tf_op | source)
XLA Modules:
  0.0 51.5 jit_solution(61949077132951143)
XLA Ops:
  0.6 2.3 %shard_map.67 = bf16[32,32,256]{2,1,0:T(8,128)(2,1)} custom-call(bf16[256,512]{1,0:T(8,128)(2,1)} %bitcast.9, bf16[256,512]{1,0:T(8,128)(2,1)} %bitcast.12, bf16[256,512]{1,0:T(8,128)(2,1)} %bitcast.13), custom_call_target="tpu_custom_call" | custom-call | bytes 1048576 | tf_op jit(solution)/shard_map/pallas_call | solution.py:332
  3.0 0.0 copy-start.1
  3.0 7.3 %all-to-all-start = ((bf16[32,32,256]{2,1,0:T(8,128)(2,1)}), bf16[32,32,256]{2,1,0:T(8,128)(2,1)S(1)}, u32[]{:S(2)}, u32[]{:S(2)}) async-start(bf16[32,32,256]{2,1,0:T(8,128)(2,1)} %shard_map.67), calls=%async_computation | async-start | bytes 1048576 | tf_op jit(solution)/shard_map/all_to_all | solution.py:346
  10.3 0.0 copy-done.1
  10.5 1.8 %collective-permute-start = (f32[1,16,16,128]{3,2,1,0:T(8,128)S(1)}, f32[1,16,16,128]{3,2,1,0:T(8,128)S(1)}, u32[]{:S(2)}, u32[]{:S(2)}) collective-permute-start(f32[1,16,16,128]{3,2,1,0:T(8,128)S(1)} %get-tuple-element.9), channel_id=1, source_target_pairs={{0,16},{16,0},{1,17},{17,1},{2,18},{18,2},{3,19},{19,3},{4,20},{20... | collective-permute-start | bytes 393224 | tf_op jit(solution)/shard_map/ppermute | solution.py:296
  12.3 7.6 %collective-permute-done = f32[1,16,16,128]{3,2,1,0:T(8,128)S(1)} collective-permute-done((f32[1,16,16,128]{3,2,1,0:T(8,128)S(1)}, f32[1,16,16,128]{3,2,1,0:T(8,128)S(1)}, u32[]{:S(2)}, u32[]{:S(2)}) %collective-permute-start) | collective-permute-done | bytes 131104 | tf_op jit(solution)/shard_map/ppermute | solution.py:296
  19.9 6.3 %all-to-all-done.got = bf16[32,32,256]{2,1,0:T(8,128)(2,1)S(1)} async-done(((bf16[32,32,256]{2,1,0:T(8,128)(2,1)}), bf16[32,32,256]{2,1,0:T(8,128)(2,1)S(1)}, u32[]{:S(2)}, u32[]{:S(2)}) %all-to-all-start) | async-done | bytes 524320 | tf_op jit(solution)/shard_map/all_to_all | solution.py:346
  26.2 5.7 %shard_map.68 = bf16[32,32,256]{2,1,0:T(8,128)(2,1)} custom-call(bf16[32,32,256]{2,1,0:T(8,128)(2,1)S(1)} %all-to-all-done.got, f32[2,16,16,128]{3,2,1,0:T(8,128)S(1)} %constant_dynamic-update-slice_fusion.1.taps), custom_call_target="tpu_custom_call" | custom-call | bytes 1048576 | tf_op jit(solution)/shard_map/pallas_call | solution.py:349
  31.9 2.6 %all-to-all-start.1 = ((bf16[32,32,256]{2,1,0:T(8,128)(2,1)}), bf16[32,32,256]{2,1,0:T(8,128)(2,1)S(1)}, u32[]{:S(2)}, u32[]{:S(2)}) async-start(bf16[32,32,256]{2,1,0:T(8,128)(2,1)} %shard_map.68), calls=%async_computation.1 | async-start | bytes 1048576 | tf_op jit(solution)/shard_map/all_to_all | solution.py:364
  34.6 8.7 %shard_map.70 = f32[2,16,2048]{2,1,0:T(8,128)S(1)} custom-call(bf16[32,32,256]{2,1,0:T(8,128)(2,1)S(1)} %all-to-all-done.got), custom_call_target="tpu_custom_call" | custom-call | flops 1073741824 | bytes 1048576 | tf_op jit(solution)/shard_map/pallas_call | solution.py:365
  43.4 0.0 copy-start
  43.4 1.7 %collective-permute-start.1 = (f32[1,16,2048]{2,1,0:T(8,128)S(1)}, f32[1,16,2048]{2,1,0:T(8,128)S(1)}, u32[]{:S(2)}, u32[]{:S(2)}) collective-permute-start(f32[1,16,2048]{2,1,0:T(8,128)S(1)} %get-tuple-element.7), channel_id=1, source_target_pairs={{0,16},{16,0},{1,17},{17,1},{2,18},{18,2},{3,19},{19,3},{4,20},{20... | collective-permute-start | bytes 393224 | tf_op jit(solution)/shard_map/ppermute | solution.py:296
  45.1 4.8 %collective-permute-done.1 = f32[1,16,2048]{2,1,0:T(8,128)S(1)} collective-permute-done((f32[1,16,2048]{2,1,0:T(8,128)S(1)}, f32[1,16,2048]{2,1,0:T(8,128)S(1)}, u32[]{:S(2)}, u32[]{:S(2)}) %collective-permute-start.1) | collective-permute-done | bytes 131104 | tf_op jit(solution)/shard_map/ppermute | solution.py:296
  49.9 0.0 copy-start.2
  49.9 0.5 all-to-all-done.1.got
  50.4 0.0 copy-done
  50.4 1.1 %shard_map.69 = (bf16[256,512]{1,0:T(8,128)(2,1)}, bf16[256,512]{1,0:T(8,128)(2,1)}) custom-call(bf16[32,32,256]{2,1,0:T(8,128)(2,1)S(1)} %all-to-all-done.1.got, bf16[256,512]{1,0:T(8,128)(2,1)S(1)} %bitcast.10), custom_call_target="tpu_custom_call" | custom-call | bytes 1048576 | tf_op jit(solution)/shard_map/pallas_call | solution.py:381
  51.5 0.0 copy-done.2
  (7 shorter events, 0.2 us)
Async XLA Ops:
  3.0 7.4 %copy-start.1 = (f32[2,16,2048]{2,1,0:T(8,128)S(1)}, f32[2,16,2048]{2,1,0:T(8,128)}, u32[]{:S(2)}) copy-start(f32[2,16,2048]{2,1,0:T(8,128)} %param.7) | copy-start | bytes 786436
  3.0 23.2 %all-to-all-start = ((bf16[32,32,256]{2,1,0:T(8,128)(2,1)}), bf16[32,32,256]{2,1,0:T(8,128)(2,1)S(1)}, u32[]{:S(2)}, u32[]{:S(2)}) async-start(bf16[32,32,256]{2,1,0:T(8,128)(2,1)} %shard_map.67), calls=%async_computation | async-start | bytes 1048576 | tf_op jit(solution)/shard_map/all_to_all | solution.py:346
  10.5 9.4 %collective-permute-start = (f32[1,16,16,128]{3,2,1,0:T(8,128)S(1)}, f32[1,16,16,128]{3,2,1,0:T(8,128)S(1)}, u32[]{:S(2)}, u32[]{:S(2)}) collective-permute-start(f32[1,16,16,128]{3,2,1,0:T(8,128)S(1)} %get-tuple-element.9), channel_id=1, source_target_pairs={{0,16},{16,0},{1,17},{17,1},{2,18},{18,2},{3,19},{19,3},{4,20},{20... | collective-permute-start | bytes 393224 | tf_op jit(solution)/shard_map/ppermute | solution.py:296
  31.9 18.5 %all-to-all-start.1 = ((bf16[32,32,256]{2,1,0:T(8,128)(2,1)}), bf16[32,32,256]{2,1,0:T(8,128)(2,1)S(1)}, u32[]{:S(2)}, u32[]{:S(2)}) async-start(bf16[32,32,256]{2,1,0:T(8,128)(2,1)} %shard_map.68), calls=%async_computation.1 | async-start | bytes 1048576 | tf_op jit(solution)/shard_map/all_to_all | solution.py:364
  43.4 7.1 %copy-start = (bf16[1,256,512]{2,1,0:T(8,128)(2,1)S(1)}, bf16[1,256,512]{2,1,0:T(8,128)(2,1)}, u32[]{:S(2)}) copy-start(bf16[1,256,512]{2,1,0:T(8,128)(2,1)} %param.4) | copy-start | bytes 786436
  43.4 6.5 %collective-permute-start.1 = (f32[1,16,2048]{2,1,0:T(8,128)S(1)}, f32[1,16,2048]{2,1,0:T(8,128)S(1)}, u32[]{:S(2)}, u32[]{:S(2)}) collective-permute-start(f32[1,16,2048]{2,1,0:T(8,128)S(1)} %get-tuple-element.7), channel_id=1, source_target_pairs={{0,16},{16,0},{1,17},{17,1},{2,18},{18,2},{3,19},{19,3},{4,20},{20... | collective-permute-start | bytes 393224 | tf_op jit(solution)/shard_map/ppermute | solution.py:296
  49.9 1.6 %copy-start.2 = (f32[2,16,2048]{2,1,0:T(8,128)}, f32[2,16,2048]{2,1,0:T(8,128)S(1)}, u32[]{:S(2)}) copy-start(f32[2,16,2048]{2,1,0:T(8,128)S(1)} %constant_dynamic-update-slice_fusion) | copy-start | bytes 786436

commit v3 on v2

--- a/solution.py
+++ b/solution.py
@@ -10,6 +10,7 @@
 LANES = 128
 PACK = 16
 AHEAD = 2
+NEAR = 2
 bf16 = jnp.bfloat16
 f32 = jnp.float32
 
@@ -120,7 +121,7 @@
     return pltpu.roll(value, 0, 1, stride=1, stride_axis=0)
 
 
-def mix_kernel(sizes, got, taps, made, plain, turned, line, shifted, result, out, done, left):
+def mix_kernel(sizes, got, taps, made, plain, turned, line, shifted, windows, result, out, done, left):
     dp, seq, cpd = sizes
     tokens = got.shape[2]
     streams = 2 * dp
@@ -143,7 +144,7 @@
     low = iota((seq, LANES), 1) < small
     order = [(k, b, half) for k in range(2) for b in range(dp) for half in range(2)]
 
-    def channel(c, u):
+    def build(c, u):
         for kind, b, half in order:
             stream = kind * dp + b
             here = held[kind][half, pl.ds(slots(b, seq, pitch) + c, seq, stride=pitch), :]
@@ -155,21 +156,22 @@
         for q in range(seq):
             shifted[u, size + q * group : size + (q + 1) * group] = line[u, pl.ds(q * (group + 1), group), :].astype(bf16)
         before = jnp.zeros((small, LANES), bf16)
+        for d in range(2 * seq):
+            row = taps[d // per_part, c, pl.ds(d % per_part, 1), :]
+            now = skew(jnp.broadcast_to(row, (small, LANES))).astype(bf16)
+            windows[u, d % 2, pl.ds((d // 2) * small, small), :] = jnp.where(lower, now, before)
+            before = now
+
+    def apply(c, u):
+        deep = seq * small // 2
         sums = []
         for which in range(2):
-            blocks, tiles = [], []
+            blocks = []
             count = size >> which
             for f in range(which * seq // 4, (which + 1) * seq // 4):
                 blocks.append(shifted[u, pl.ds(2 * size - count - 2 * f * group, count), :])
-                pieces = []
-                for d in range(4 * f, 4 * f + 4):
-                    row = taps[d // per_part, c, pl.ds(d % per_part, 1), :]
-                    now = skew(jnp.broadcast_to(row, (small, LANES))).astype(bf16)
-                    pieces.append(jnp.where(lower, now, before))
-                    before = now
-                tiles.append(jnp.concatenate(pieces[:2], axis=1))
-                tiles.append(jnp.concatenate(pieces[2:], axis=1))
-            sums.append(times(jnp.concatenate(blocks, axis=1), jnp.concatenate(tiles, axis=0)))
+            tiles = [windows[u, k, pl.ds(which * deep, deep), :] for k in range(2)]
+            sums.append(times(jnp.concatenate(blocks, axis=1), jnp.concatenate(tiles, axis=1)))
         total = jnp.concatenate([sums[0][: size // 2], sums[0][size // 2 :] + sums[1]], axis=0)
         rows = 2 * streams
         late = jnp.concatenate([jnp.zeros((rows, LANES), f32), total[: size - rows, LANES:]], axis=0)
@@ -188,15 +190,12 @@
 
     parts = left.shape[0]
     each = cpd // parts
-    going = []
-    for part in range(parts):
-
-        def step(i, carry):
-            for u in range(ahead):
-                channel(part * each + i * ahead + u, u)
-            return carry
-
-        lax.fori_loop(0, each // ahead, step, 0)
+
+    def going(part, kind):
+        to = pl.ds(kind * cpd + part * each, each)
+        return pltpu.make_async_copy(done.at[:, to, :], made.at[:, to, :], left.at[part, kind])
+
+    def finish(part):
         for kind in range(2):
             to = pl.ds(kind * cpd + part * each, each)
             for b in range(dp):
@@ -204,10 +203,33 @@
                     at = pl.ds((b * seq + q) * pitch + part * each, each)
                     value = jnp.concatenate([out[kind, half, at, :] for half in range(2)], axis=1)
                     done[b * seq + (seq - 1 - q if kind else q), to, :] = value.astype(bf16)
-            going.append(pltpu.make_async_copy(done.at[:, to, :], made.at[:, to, :], left.at[part, kind]))
-            going[-1].start()
-    for copy in going:
-        copy.wait()
+            going(part, kind).start()
+
+    near = ahead // 2
+    pairs = cpd // ahead
+
+    def each_of(work, first, side):
+        for u in range(near):
+            work(first + u, side * near + u)
+
+    def step(k, carry):
+        if parts > 1:
+            pl.when(k == pairs // parts)(lambda: finish(0))
+        each_of(build, k * ahead + near, 1)
+        each_of(apply, k * ahead, 0)
+        each_of(build, k * ahead + ahead, 0)
+        each_of(apply, k * ahead + near, 1)
+        return carry
+
+    each_of(build, 0, 0)
+    lax.fori_loop(0, pairs - 1, step, 0)
+    each_of(build, cpd - near, 1)
+    each_of(apply, cpd - ahead, 0)
+    each_of(apply, cpd - near, 1)
+    finish(parts - 1)
+    for part in range(parts):
+        for kind in range(2):
+            going(part, kind).wait()
 
 
 def tap_kernel(sizes, factor, got, made, mirrored, turned, line, flat, shifted, square, partial, lags):
@@ -298,7 +320,7 @@
     return result
 
 
-def call(kernel, out_shape, scratch=(), flops=0, limit=16, specs=None):
+def call(kernel, out_shape, scratch=(), flops=0, limit=24, specs=None):
     extra = {} if specs is None else dict(in_specs=specs[0], out_specs=specs[1])
     return pl.pallas_call(
         kernel,
@@ -324,7 +346,7 @@
     slot_rows = dp * (seq + 1) * (cpd + 1)
     line_rows = seq * (2 * streams + 1)
     ahead = AHEAD if cpd % AHEAD == 0 else 1
-    many = 4 if cpd % 16 == 0 else ahead
+    many = 2 * NEAR if cpd % (2 * NEAR) == 0 else 2
     both = ("dp", "seq")
     taps = exchange(filters.reshape(dp, cpd, part // LANES, LANES), "dp")
     edge = (dp, seq, per, spd)
@@ -345,7 +367,7 @@
     )(grad_out[0], gate[0], signal[0])
     got = lax.all_to_all(sent, both, split_axis=0, concat_axis=0, tiled=True)
     inner = (dp, seq, cpd)
-    parts = 2 if cpd % 16 == 0 else 1
+    parts = 2 if cpd % (4 * many) == 0 else 1
     made = call(
         functools.partial(mix_kernel, inner),
         shape((dp * seq, 2 * cpd, tokens), bf16),
@@ -354,6 +376,7 @@
             pltpu.VMEM((2, slot_rows, LANES), f32),
             pltpu.VMEM((many, seq * (group + 1), LANES), f32),
             pltpu.VMEM((many, 2 * seq * group, LANES), bf16),
+            pltpu.VMEM((many, 2, seq * LANES // 2, LANES), bf16),
             pltpu.VMEM((many, 2, line_rows + 2 * streams + 1, LANES), f32),
             pltpu.VMEM((2, 2, dp * seq * (cpd + 1), LANES), f32),
             pltpu.VMEM((dp * seq, 2 * cpd, tokens), bf16),

time: 51.9 us -> 50.7 us (0.977)
  Pallas kernels: 17.9 us -> 16.7 us
    pallas_call x1, Pallas kernels: 5.74 us -> 4.56 us  [on_device(): call(functools.partial(mix_kernel, inner), shape((dp * seq, 2 * cpd, toke...]
where the time goes in v3:
time: 50.7 us; the launch traced here: 50.3 us
  waiting for transfers between devices  19.2 us (38%)
  Pallas kernels  16.7 us (33%)
  starting transfers between devices  13.5 us (27%)
  between operations  0.77 us (2%)
    ppermute x2, waiting for transfers between devices, exchange(): part = lax.ppermute(part, axis, [(i, (i + k) % size) for i in range(size)])  12.4 us
    pallas_call x1, Pallas kernels, on_device(): call(functools.partial(tap_kernel, inner, float(dp * length) ** (-0.5)),...  8.75 us
    all_to_all x1, starting transfers between devices, on_device(): got = lax.all_to_all(sent, both, split_axis=0, concat_axis=0, tiled=True)  7.33 us
    all_to_all x1, waiting for transfers between devices, on_device(): got = lax.all_to_all(sent, both, split_axis=0, concat_axis=0, tiled=True)  6.26 us
    pallas_call x1, Pallas kernels, on_device(): call(functools.partial(mix_kernel, inner), shape((dp * seq, 2 * cpd, toke...  4.56 us
    ppermute x2, starting transfers between devices, exchange(): part = lax.ppermute(part, axis, [(i, (i + k) % size) for i in range(size)])  3.54 us
    all_to_all x1, starting transfers between devices, on_device(): back = lax.all_to_all(made, both, split_axis=0, concat_axis=0, tiled=True)  2.62 us
    pallas_call x1, Pallas kernels, on_device(): call(functools.partial(send_kernel, edge), shape((dp * seq, 2 * cpd, toke...  2.32 us
  transfers between devices with their start and end apart: 4, of which 4 were waited for; matrix products, arithmetic and copies ran while one was open for 0% of the time, Pallas kernels for 17%

profile of v3, /device:TPU:0, one launch (start us, length us, event | category | flops | bytes accessed | tf_op | source)
XLA Modules:
  0.0 50.3 jit_solution(17465878047876581182)
XLA Ops:
  0.6 2.3 %shard_map.67 = bf16[32,32,256]{2,1,0:T(8,128)(2,1)} custom-call(bf16[256,512]{1,0:T(8,128)(2,1)} %bitcast.9, bf16[256,512]{1,0:T(8,128)(2,1)} %bitcast.12, bf16[256,512]{1,0:T(8,128)(2,1)} %bitcast.13), custom_call_target="tpu_custom_call" | custom-call | bytes 1048576 | tf_op jit(solution)/shard_map/pallas_call | solution.py:354
  3.0 0.0 copy-start.1
  3.0 7.3 %all-to-all-start = ((bf16[32,32,256]{2,1,0:T(8,128)(2,1)}), bf16[32,32,256]{2,1,0:T(8,128)(2,1)S(1)}, u32[]{:S(2)}, u32[]{:S(2)}) async-start(bf16[32,32,256]{2,1,0:T(8,128)(2,1)} %shard_map.67), calls=%async_computation | async-start | bytes 1048576 | tf_op jit(solution)/shard_map/all_to_all | solution.py:368
  10.3 0.0 copy-done.1
  10.5 1.8 %collective-permute-start = (f32[1,16,16,128]{3,2,1,0:T(8,128)S(1)}, f32[1,16,16,128]{3,2,1,0:T(8,128)S(1)}, u32[]{:S(2)}, u32[]{:S(2)}) collective-permute-start(f32[1,16,16,128]{3,2,1,0:T(8,128)S(1)} %get-tuple-element.9), channel_id=1, source_target_pairs={{0,16},{16,0},{1,17},{17,1},{2,18},{18,2},{3,19},{19,3},{4,20},{20... | collective-permute-start | bytes 393224 | tf_op jit(solution)/shard_map/ppermute | solution.py:318
  12.3 7.6 %collective-permute-done = f32[1,16,16,128]{3,2,1,0:T(8,128)S(1)} collective-permute-done((f32[1,16,16,128]{3,2,1,0:T(8,128)S(1)}, f32[1,16,16,128]{3,2,1,0:T(8,128)S(1)}, u32[]{:S(2)}, u32[]{:S(2)}) %collective-permute-start) | collective-permute-done | bytes 131104 | tf_op jit(solution)/shard_map/ppermute | solution.py:318
  19.9 6.3 %all-to-all-done.got = bf16[32,32,256]{2,1,0:T(8,128)(2,1)S(1)} async-done(((bf16[32,32,256]{2,1,0:T(8,128)(2,1)}), bf16[32,32,256]{2,1,0:T(8,128)(2,1)S(1)}, u32[]{:S(2)}, u32[]{:S(2)}) %all-to-all-start) | async-done | bytes 524320 | tf_op jit(solution)/shard_map/all_to_all | solution.py:368
  26.2 4.6 %shard_map.68 = bf16[32,32,256]{2,1,0:T(8,128)(2,1)} custom-call(bf16[32,32,256]{2,1,0:T(8,128)(2,1)S(1)} %all-to-all-done.got, f32[2,16,16,128]{3,2,1,0:T(8,128)S(1)} %constant_dynamic-update-slice_fusion.1.taps), custom_call_target="tpu_custom_call" | custom-call | bytes 1048576 | tf_op jit(solution)/shard_map/pallas_call | solution.py:371
  30.7 2.6 %all-to-all-start.1 = ((bf16[32,32,256]{2,1,0:T(8,128)(2,1)}), bf16[32,32,256]{2,1,0:T(8,128)(2,1)S(1)}, u32[]{:S(2)}, u32[]{:S(2)}) async-start(bf16[32,32,256]{2,1,0:T(8,128)(2,1)} %shard_map.68), calls=%async_computation.1 | async-start | bytes 1048576 | tf_op jit(solution)/shard_map/all_to_all | solution.py:387
  33.4 8.7 %shard_map.70 = f32[2,16,2048]{2,1,0:T(8,128)S(1)} custom-call(bf16[32,32,256]{2,1,0:T(8,128)(2,1)S(1)} %all-to-all-done.got), custom_call_target="tpu_custom_call" | custom-call | flops 1073741824 | bytes 1048576 | tf_op jit(solution)/shard_map/pallas_call | solution.py:388
  42.2 0.0 copy-start
  42.2 1.7 %collective-permute-start.1 = (f32[1,16,2048]{2,1,0:T(8,128)S(1)}, f32[1,16,2048]{2,1,0:T(8,128)S(1)}, u32[]{:S(2)}, u32[]{:S(2)}) collective-permute-start(f32[1,16,2048]{2,1,0:T(8,128)S(1)} %get-tuple-element.7), channel_id=1, source_target_pairs={{0,16},{16,0},{1,17},{17,1},{2,18},{18,2},{3,19},{19,3},{4,20},{20... | collective-permute-start | bytes 393224 | tf_op jit(solution)/shard_map/ppermute | solution.py:318
  43.9 4.8 %collective-permute-done.1 = f32[1,16,2048]{2,1,0:T(8,128)S(1)} collective-permute-done((f32[1,16,2048]{2,1,0:T(8,128)S(1)}, f32[1,16,2048]{2,1,0:T(8,128)S(1)}, u32[]{:S(2)}, u32[]{:S(2)}) %collective-permute-start.1) | collective-permute-done | bytes 131104 | tf_op jit(solution)/shard_map/ppermute | solution.py:318
  48.7 0.0 copy-start.2
  48.7 0.5 all-to-all-done.1.got
  49.2 0.0 copy-done
  49.3 1.1 %shard_map.69 = (bf16[256,512]{1,0:T(8,128)(2,1)}, bf16[256,512]{1,0:T(8,128)(2,1)}) custom-call(bf16[32,32,256]{2,1,0:T(8,128)(2,1)S(1)} %all-to-all-done.1.got, bf16[256,512]{1,0:T(8,128)(2,1)S(1)} %bitcast.10), custom_call_target="tpu_custom_call" | custom-call | bytes 1048576 | tf_op jit(solution)/shard_map/pallas_call | solution.py:404
  50.3 0.0 copy-done.2
  (7 shorter events, 0.2 us)
Async XLA Ops:
  3.0 7.4 %copy-start.1 = (f32[2,16,2048]{2,1,0:T(8,128)S(1)}, f32[2,16,2048]{2,1,0:T(8,128)}, u32[]{:S(2)}) copy-start(f32[2,16,2048]{2,1,0:T(8,128)} %param.7) | copy-start | bytes 786436
  3.0 23.2 %all-to-all-start = ((bf16[32,32,256]{2,1,0:T(8,128)(2,1)}), bf16[32,32,256]{2,1,0:T(8,128)(2,1)S(1)}, u32[]{:S(2)}, u32[]{:S(2)}) async-start(bf16[32,32,256]{2,1,0:T(8,128)(2,1)} %shard_map.67), calls=%async_computation | async-start | bytes 1048576 | tf_op jit(solution)/shard_map/all_to_all | solution.py:368
  10.5 9.4 %collective-permute-start = (f32[1,16,16,128]{3,2,1,0:T(8,128)S(1)}, f32[1,16,16,128]{3,2,1,0:T(8,128)S(1)}, u32[]{:S(2)}, u32[]{:S(2)}) collective-permute-start(f32[1,16,16,128]{3,2,1,0:T(8,128)S(1)} %get-tuple-element.9), channel_id=1, source_target_pairs={{0,16},{16,0},{1,17},{17,1},{2,18},{18,2},{3,19},{19,3},{4,20},{20... | collective-permute-start | bytes 393224 | tf_op jit(solution)/shard_map/ppermute | solution.py:318
  30.7 18.5 %all-to-all-start.1 = ((bf16[32,32,256]{2,1,0:T(8,128)(2,1)}), bf16[32,32,256]{2,1,0:T(8,128)(2,1)S(1)}, u32[]{:S(2)}, u32[]{:S(2)}) async-start(bf16[32,32,256]{2,1,0:T(8,128)(2,1)} %shard_map.68), calls=%async_computation.1 | async-start | bytes 1048576 | tf_op jit(solution)/shard_map/all_to_all | solution.py:387
  42.2 7.1 %copy-start = (bf16[1,256,512]{2,1,0:T(8,128)(2,1)S(1)}, bf16[1,256,512]{2,1,0:T(8,128)(2,1)}, u32[]{:S(2)}) copy-start(bf16[1,256,512]{2,1,0:T(8,128)(2,1)} %param.4) | copy-start | bytes 786436
  42.2 6.5 %collective-permute-start.1 = (f32[1,16,2048]{2,1,0:T(8,128)S(1)}, f32[1,16,2048]{2,1,0:T(8,128)S(1)}, u32[]{:S(2)}, u32[]{:S(2)}) collective-permute-start(f32[1,16,2048]{2,1,0:T(8,128)S(1)} %get-tuple-element.7), channel_id=1, source_target_pairs={{0,16},{16,0},{1,17},{17,1},{2,18},{18,2},{3,19},{19,3},{4,20},{20... | collective-permute-start | bytes 393224 | tf_op jit(solution)/shard_map/ppermute | solution.py:318
  48.7 1.6 %copy-start.2 = (f32[2,16,2048]{2,1,0:T(8,128)}, f32[2,16,2048]{2,1,0:T(8,128)S(1)}, u32[]{:S(2)}) copy-start(f32[2,16,2048]{2,1,0:T(8,128)S(1)} %constant_dynamic-update-slice_fusion) | copy-start | bytes 786436

commit v4 on v3

--- a/solution.py
+++ b/solution.py
@@ -121,7 +121,32 @@
     return pltpu.roll(value, 0, 1, stride=1, stride_axis=0)
 
 
-def mix_kernel(sizes, got, taps, made, plain, turned, line, shifted, windows, result, out, done, left):
+def filter_windows(taps, c, seq, lower, store):
+    per_part = taps.shape[2]
+    small = LANES // 2
+    before = jnp.zeros((small, LANES), bf16)
+    for d in range(2 * seq):
+        row = taps[d // per_part, c, pl.ds(d % per_part, 1), :]
+        now = skew(jnp.broadcast_to(row, (small, LANES))).astype(bf16)
+        store(d % 2, pl.ds((d // 2) * small, small), jnp.where(lower, now, before))
+        before = now
+
+
+def window_kernel(seq, taps, made):
+    small = LANES // 2
+    lower = iota((small, LANES), 1) >= iota((small, LANES), 0)
+
+    def channel(c, carry):
+        def store(k, rows, value):
+            made[c, k, rows, :] = value
+
+        filter_windows(taps, c, seq, lower, store)
+        return carry
+
+    lax.fori_loop(0, made.shape[0], channel, 0)
+
+
+def mix_kernel(sizes, got, taps, ready, made, plain, turned, line, shifted, windows, result, out, done, left):
     dp, seq, cpd = sizes
     tokens = got.shape[2]
     streams = 2 * dp
@@ -132,7 +157,6 @@
     pitch = cpd + 1
     ahead = line.shape[0]
 
-    per_part = taps.shape[2]
     held = (plain, turned)
     stage(dp, seq, cpd, got, plain, turned)
     for one in held:
@@ -144,7 +168,7 @@
     low = iota((seq, LANES), 1) < small
     order = [(k, b, half) for k in range(2) for b in range(dp) for half in range(2)]
 
-    def build(c, u):
+    def build(c, u, early=False):
         for kind, b, half in order:
             stream = kind * dp + b
             here = held[kind][half, pl.ds(slots(b, seq, pitch) + c, seq, stride=pitch), :]
@@ -155,14 +179,14 @@
             line[u, pl.ds(to + streams, seq, stride=group + 1), :] = jnp.where(low, crossed, behind)
         for q in range(seq):
             shifted[u, size + q * group : size + (q + 1) * group] = line[u, pl.ds(q * (group + 1), group), :].astype(bf16)
-        before = jnp.zeros((small, LANES), bf16)
-        for d in range(2 * seq):
-            row = taps[d // per_part, c, pl.ds(d % per_part, 1), :]
-            now = skew(jnp.broadcast_to(row, (small, LANES))).astype(bf16)
-            windows[u, d % 2, pl.ds((d // 2) * small, small), :] = jnp.where(lower, now, before)
-            before = now
-
-    def apply(c, u):
+        if not early:
+
+            def store(k, rows, value):
+                windows[u, k, rows, :] = value
+
+            filter_windows(taps, c, seq, lower, store)
+
+    def apply(c, u, early=False):
         deep = seq * small // 2
         sums = []
         for which in range(2):
@@ -170,7 +194,8 @@
             count = size >> which
             for f in range(which * seq // 4, (which + 1) * seq // 4):
                 blocks.append(shifted[u, pl.ds(2 * size - count - 2 * f * group, count), :])
-            tiles = [windows[u, k, pl.ds(which * deep, deep), :] for k in range(2)]
+            source, at = (ready, c) if early else (windows, u)
+            tiles = [source[at, k, pl.ds(which * deep, deep), :] for k in range(2)]
             sums.append(times(jnp.concatenate(blocks, axis=1), jnp.concatenate(tiles, axis=1)))
         total = jnp.concatenate([sums[0][: size // 2], sums[0][size // 2 :] + sums[1]], axis=0)
         rows = 2 * streams
@@ -208,9 +233,9 @@
     near = ahead // 2
     pairs = cpd // ahead
 
-    def each_of(work, first, side):
+    def each_of(work, first, side, early=False):
         for u in range(near):
-            work(first + u, side * near + u)
+            work(first + u, side * near + u, early)
 
     def step(k, carry):
         if parts > 1:
@@ -221,8 +246,14 @@
         each_of(apply, k * ahead + near, 1)
         return carry
 
-    each_of(build, 0, 0)
-    lax.fori_loop(0, pairs - 1, step, 0)
+    begin = ready.shape[0] // ahead
+    each_of(build, 0, 0, begin > 0)
+    if begin:
+        each_of(build, near, 1, True)
+        each_of(apply, 0, 0, True)
+        each_of(build, ahead, 0)
+        each_of(apply, near, 1, True)
+    lax.fori_loop(begin, pairs - 1, step, 0)
     each_of(build, cpd - near, 1)
     each_of(apply, cpd - ahead, 0)
     each_of(apply, cpd - near, 1)
@@ -367,6 +398,13 @@
     )(grad_out[0], gate[0], signal[0])
     got = lax.all_to_all(sent, both, split_axis=0, concat_axis=0, tiled=True)
     inner = (dp, seq, cpd)
+    pairs = cpd // many
+    ready = call(
+        functools.partial(window_kernel, seq),
+        shape((many if pairs > 2 else 1, 2, seq * LANES // 2, LANES), bf16),
+        flops=1 << 30,
+        specs=([pl.BlockSpec(memory_space=pltpu.VMEM)], pl.BlockSpec(memory_space=pltpu.VMEM)),
+    )(taps)
     parts = 2 if cpd % (4 * many) == 0 else 1
     made = call(
         functools.partial(mix_kernel, inner),
@@ -382,8 +420,8 @@
             pltpu.VMEM((dp * seq, 2 * cpd, tokens), bf16),
             pltpu.SemaphoreType.DMA((parts, 2)),
         ),
-        specs=([pl.BlockSpec(memory_space=pltpu.VMEM)] * 2, anywhere),
-    )(got, taps)
+        specs=([pl.BlockSpec(memory_space=pltpu.VMEM)] * 3, anywhere),
+    )(got, taps, ready)
     back = lax.all_to_all(made, both, split_axis=0, concat_axis=0, tiled=True)
     lags = call(
         functools.partial(tap_kernel, inner, float(dp * length) ** -0.5),

time: 50.7 us -> 50.2 us (level)
  waiting for transfers between devices: 19.2 us -> 18.3 us
    all_to_all x1, waiting for transfers between devices: 6.26 us -> 5.42 us  [on_device(): got = lax.all_to_all(sent, both, split_axis=0, concat_axis=0, tiled=True)]
    pallas_call x0 -> x1, Pallas kernels: none -> 0.83 us  [on_device(): call(functools.partial(window_kernel, seq), shape((many if pairs > 2 else...]
  transfers between devices with their start and end apart: 4 -> 4, of which waited for: 4 -> 4; matrix products, arithmetic and copies ran while one was open for 0% -> 0% of each run, Pallas kernels for 17% -> 19%
where the time goes in v4:
time: 50.2 us; the launch traced here: 49.9 us
  waiting for transfers between devices  18.3 us (36%)
  Pallas kernels  17.1 us (34%)
  starting transfers between devices  13.5 us (27%)
  between operations  0.78 us (2%)
    ppermute x2, waiting for transfers between devices, exchange(): part = lax.ppermute(part, axis, [(i, (i + k) % size) for i in range(size)])  12.4 us
    pallas_call x1, Pallas kernels, on_device(): call(functools.partial(tap_kernel, inner, float(dp * length) ** (-0.5)),...  8.75 us
    all_to_all x1, starting transfers between devices, on_device(): got = lax.all_to_all(sent, both, split_axis=0, concat_axis=0, tiled=True)  7.33 us
    all_to_all x1, waiting for transfers between devices, on_device(): got = lax.all_to_all(sent, both, split_axis=0, concat_axis=0, tiled=True)  5.42 us
    pallas_call x1, Pallas kernels, on_device(): call(functools.partial(mix_kernel, inner), shape((dp * seq, 2 * cpd, toke...  4.1 us
    ppermute x2, starting transfers between devices, exchange(): part = lax.ppermute(part, axis, [(i, (i + k) % size) for i in range(size)])  3.53 us
    all_to_all x1, starting transfers between devices, on_device(): back = lax.all_to_all(made, both, split_axis=0, concat_axis=0, tiled=True)  2.62 us
    pallas_call x1, Pallas kernels, on_device(): call(functools.partial(send_kernel, edge), shape((dp * seq, 2 * cpd, toke...  2.36 us
  transfers between devices with their start and end apart: 4, of which 4 were waited for; matrix products, arithmetic and copies ran while one was open for 0% of the time, Pallas kernels for 19%

profile of v4, /device:TPU:0, one launch (start us, length us, event | category | flops | bytes accessed | tf_op | source)
XLA Modules:
  0.0 49.9 jit_solution(14156175967750826164)
XLA Ops:
  0.6 0.0 copy-start.1
  0.6 2.4 %shard_map.67 = bf16[32,32,256]{2,1,0:T(8,128)(2,1)} custom-call(bf16[256,512]{1,0:T(8,128)(2,1)} %bitcast.9, bf16[256,512]{1,0:T(8,128)(2,1)} %bitcast.12, bf16[256,512]{1,0:T(8,128)(2,1)} %bitcast.13), custom_call_target="tpu_custom_call" | custom-call | bytes 1048576 | tf_op jit(solution)/shard_map/pallas_call | solution.py:385
  3.0 7.3 %all-to-all-start = ((bf16[32,32,256]{2,1,0:T(8,128)(2,1)}), bf16[32,32,256]{2,1,0:T(8,128)(2,1)S(1)}, u32[]{:S(2)}, u32[]{:S(2)}) async-start(bf16[32,32,256]{2,1,0:T(8,128)(2,1)} %shard_map.67), calls=%async_computation | async-start | bytes 1048576 | tf_op jit(solution)/shard_map/all_to_all | solution.py:399
  10.4 0.0 copy-done.1
  10.5 1.8 %collective-permute-start = (f32[1,16,16,128]{3,2,1,0:T(8,128)S(1)}, f32[1,16,16,128]{3,2,1,0:T(8,128)S(1)}, u32[]{:S(2)}, u32[]{:S(2)}) collective-permute-start(f32[1,16,16,128]{3,2,1,0:T(8,128)S(1)} %get-tuple-element.9), channel_id=1, source_target_pairs={{0,16},{16,0},{1,17},{17,1},{2,18},{18,2},{3,19},{19,3},{4,20},{20... | collective-permute-start | bytes 393224 | tf_op jit(solution)/shard_map/ppermute | solution.py:349
  12.3 7.6 %collective-permute-done = f32[1,16,16,128]{3,2,1,0:T(8,128)S(1)} collective-permute-done((f32[1,16,16,128]{3,2,1,0:T(8,128)S(1)}, f32[1,16,16,128]{3,2,1,0:T(8,128)S(1)}, u32[]{:S(2)}, u32[]{:S(2)}) %collective-permute-start) | collective-permute-done | bytes 131104 | tf_op jit(solution)/shard_map/ppermute | solution.py:349
  20.0 0.8 %shard_map.68.ready = bf16[4,2,1024,128]{3,2,1,0:T(8,128)(2,1)S(1)} custom-call(f32[2,16,16,128]{3,2,1,0:T(8,128)S(1)} %constant_dynamic-update-slice_fusion.1.taps), custom_call_target="tpu_custom_call" | custom-call | flops 1073741824 | bytes 1048576 | tf_op jit(solution)/shard_map/pallas_call | solution.py:402
  20.8 5.4 %all-to-all-done.got = bf16[32,32,256]{2,1,0:T(8,128)(2,1)S(1)} async-done(((bf16[32,32,256]{2,1,0:T(8,128)(2,1)}), bf16[32,32,256]{2,1,0:T(8,128)(2,1)S(1)}, u32[]{:S(2)}, u32[]{:S(2)}) %all-to-all-start) | async-done | bytes 524320 | tf_op jit(solution)/shard_map/all_to_all | solution.py:399
  26.2 4.1 %shard_map.69 = bf16[32,32,256]{2,1,0:T(8,128)(2,1)} custom-call(bf16[32,32,256]{2,1,0:T(8,128)(2,1)S(1)} %all-to-all-done.got, f32[2,16,16,128]{3,2,1,0:T(8,128)S(1)} %constant_dynamic-update-slice_fusion.1.taps, bf16[4,2,1024,128]{3,2,1,0:T(8,128)(2,1)S(1)} %shard_map.68.ready), custom_call_target="tpu_custom_call" | custom-call | bytes 1048576 | tf_op jit(solution)/shard_map/pallas_call | solution.py:409
  30.3 2.6 %all-to-all-start.1 = ((bf16[32,32,256]{2,1,0:T(8,128)(2,1)}), bf16[32,32,256]{2,1,0:T(8,128)(2,1)S(1)}, u32[]{:S(2)}, u32[]{:S(2)}) async-start(bf16[32,32,256]{2,1,0:T(8,128)(2,1)} %shard_map.69), calls=%async_computation.1 | async-start | bytes 1048576 | tf_op jit(solution)/shard_map/all_to_all | solution.py:425
  33.0 0.0 copy-start
  33.0 8.8 %shard_map.71 = f32[2,16,2048]{2,1,0:T(8,128)S(1)} custom-call(bf16[32,32,256]{2,1,0:T(8,128)(2,1)S(1)} %all-to-all-done.got), custom_call_target="tpu_custom_call" | custom-call | flops 1073741824 | bytes 1048576 | tf_op jit(solution)/shard_map/pallas_call | solution.py:426
  41.8 1.7 %collective-permute-start.1 = (f32[1,16,2048]{2,1,0:T(8,128)S(1)}, f32[1,16,2048]{2,1,0:T(8,128)S(1)}, u32[]{:S(2)}, u32[]{:S(2)}) collective-permute-start(f32[1,16,2048]{2,1,0:T(8,128)S(1)} %get-tuple-element.7), channel_id=1, source_target_pairs={{0,16},{16,0},{1,17},{17,1},{2,18},{18,2},{3,19},{19,3},{4,20},{20... | collective-permute-start | bytes 393224 | tf_op jit(solution)/shard_map/ppermute | solution.py:349
  43.5 4.8 %collective-permute-done.1 = f32[1,16,2048]{2,1,0:T(8,128)S(1)} collective-permute-done((f32[1,16,2048]{2,1,0:T(8,128)S(1)}, f32[1,16,2048]{2,1,0:T(8,128)S(1)}, u32[]{:S(2)}, u32[]{:S(2)}) %collective-permute-start.1) | collective-permute-done | bytes 131104 | tf_op jit(solution)/shard_map/ppermute | solution.py:349
  48.3 0.0 copy-start.2
  48.3 0.5 all-to-all-done.1.got
  48.8 0.0 copy-done
  48.8 1.1 %shard_map.70 = (bf16[256,512]{1,0:T(8,128)(2,1)}, bf16[256,512]{1,0:T(8,128)(2,1)}) custom-call(bf16[32,32,256]{2,1,0:T(8,128)(2,1)S(1)} %all-to-all-done.1.got, bf16[256,512]{1,0:T(8,128)(2,1)S(1)} %bitcast.10), custom_call_target="tpu_custom_call" | custom-call | bytes 1048576 | tf_op jit(solution)/shard_map/pallas_call | solution.py:442
  49.9 0.0 copy-done.2
  (7 shorter events, 0.2 us)
Async XLA Ops:
  0.6 9.7 %copy-start.1 = (f32[2,16,2048]{2,1,0:T(8,128)S(1)}, f32[2,16,2048]{2,1,0:T(8,128)}, u32[]{:S(2)}) copy-start(f32[2,16,2048]{2,1,0:T(8,128)} %param.7) | copy-start | bytes 786436
  3.0 23.2 %all-to-all-start = ((bf16[32,32,256]{2,1,0:T(8,128)(2,1)}), bf16[32,32,256]{2,1,0:T(8,128)(2,1)S(1)}, u32[]{:S(2)}, u32[]{:S(2)}) async-start(bf16[32,32,256]{2,1,0:T(8,128)(2,1)} %shard_map.67), calls=%async_computation | async-start | bytes 1048576 | tf_op jit(solution)/shard_map/all_to_all | solution.py:399
  10.5 9.4 %collective-permute-start = (f32[1,16,16,128]{3,2,1,0:T(8,128)S(1)}, f32[1,16,16,128]{3,2,1,0:T(8,128)S(1)}, u32[]{:S(2)}, u32[]{:S(2)}) collective-permute-start(f32[1,16,16,128]{3,2,1,0:T(8,128)S(1)} %get-tuple-element.9), channel_id=1, source_target_pairs={{0,16},{16,0},{1,17},{17,1},{2,18},{18,2},{3,19},{19,3},{4,20},{20... | collective-permute-start | bytes 393224 | tf_op jit(solution)/shard_map/ppermute | solution.py:349
  30.3 18.5 %all-to-all-start.1 = ((bf16[32,32,256]{2,1,0:T(8,128)(2,1)}), bf16[32,32,256]{2,1,0:T(8,128)(2,1)S(1)}, u32[]{:S(2)}, u32[]{:S(2)}) async-start(bf16[32,32,256]{2,1,0:T(8,128)(2,1)} %shard_map.69), calls=%async_computation.1 | async-start | bytes 1048576 | tf_op jit(solution)/shard_map/all_to_all | solution.py:425
  33.0 15.9 %copy-start = (bf16[1,256,512]{2,1,0:T(8,128)(2,1)S(1)}, bf16[1,256,512]{2,1,0:T(8,128)(2,1)}, u32[]{:S(2)}) copy-start(bf16[1,256,512]{2,1,0:T(8,128)(2,1)} %param.4) | copy-start | bytes 786436
  41.8 6.5 %collective-permute-start.1 = (f32[1,16,2048]{2,1,0:T(8,128)S(1)}, f32[1,16,2048]{2,1,0:T(8,128)S(1)}, u32[]{:S(2)}, u32[]{:S(2)}) collective-permute-start(f32[1,16,2048]{2,1,0:T(8,128)S(1)} %get-tuple-element.7), channel_id=1, source_target_pairs={{0,16},{16,0},{1,17},{17,1},{2,18},{18,2},{3,19},{19,3},{4,20},{20... | collective-permute-start | bytes 393224 | tf_op jit(solution)/shard_map/ppermute | solution.py:349
  48.3 1.6 %copy-start.2 = (f32[2,16,2048]{2,1,0:T(8,128)}, f32[2,16,2048]{2,1,0:T(8,128)S(1)}, u32[]{:S(2)}) copy-start(f32[2,16,2048]{2,1,0:T(8,128)S(1)} %constant_dynamic-update-slice_fusion) | copy-start | bytes 786436

commit v5 on v4

--- a/solution.py
+++ b/solution.py
@@ -37,28 +37,20 @@
     width = per * seq * spd
     pairs = ((signal, signals), (out_grad, grads), (gate, gates))
     coming = [
-        [
-            pltpu.make_async_copy(
-                source.at[:, pl.ds(p * width, width)],
-                held.at[:, pl.ds(p * width, width)],
-                arrived.at[k, p],
-            )
-            for k, (source, held) in enumerate(pairs)
-        ]
-        for p in range(dp)
+        pltpu.make_async_copy(source, held, arrived.at[k]) for k, (source, held) in enumerate(pairs)
     ]
     going = [
         pltpu.make_async_copy(made.at[pl.ds(p * seq, seq)], sent.at[pl.ds(p * seq, seq)], left.at[p])
         for p in range(dp)
     ]
-    for copies in coming:
-        for copy in copies:
-            copy.start()
+    for copy in coming:
+        copy.start()
     flip = flip_matrix(grads.shape[0], bf16)
     for p in range(dp):
         at = pl.ds(p * width, width)
-        for copy in coming[p]:
-            copy.wait()
+        if p == 0:
+            for copy in coming:
+                copy.wait()
         scaled = (grads[:, at].astype(f32) * gates[:, at].astype(f32)).T
         scaled = times(scaled.astype(bf16), flip)
         plain = signals[:, at].astype(f32).T
@@ -390,7 +382,7 @@
             pltpu.VMEM((tokens, channels), bf16),
             pltpu.VMEM((tokens, channels), bf16),
             pltpu.VMEM((dp * seq, 2 * cpd, tokens), bf16),
-            pltpu.SemaphoreType.DMA((3, dp)),
+            pltpu.SemaphoreType.DMA((3,)),
             pltpu.SemaphoreType.DMA((dp,)),
         ),
         limit=63,

time: 50.2 us -> 50.1 us (level)
  no operation moved by 1% of the time
where the time goes in v5:
time: 50.1 us; the launch traced here: 49.8 us
  waiting for transfers between devices  18.3 us (37%)
  Pallas kernels  17 us (34%)
  starting transfers between devices  13.5 us (27%)
  between operations  0.78 us (2%)
    ppermute x2, waiting for transfers between devices, exchange(): part = lax.ppermute(part, axis, [(i, (i + k) % size) for i in range(size)])  12.4 us
    pallas_call x1, Pallas kernels, on_device(): call(functools.partial(tap_kernel, inner, float(dp * length) ** (-0.5)),...  8.75 us
    all_to_all x1, starting transfers between devices, on_device(): got = lax.all_to_all(sent, both, split_axis=0, concat_axis=0, tiled=True)  7.33 us
    all_to_all x1, waiting for transfers between devices, on_device(): got = lax.all_to_all(sent, both, split_axis=0, concat_axis=0, tiled=True)  5.42 us
    pallas_call x1, Pallas kernels, on_device(): call(functools.partial(mix_kernel, inner), shape((dp * seq, 2 * cpd, toke...  4.11 us
    ppermute x2, starting transfers between devices, exchange(): part = lax.ppermute(part, axis, [(i, (i + k) % size) for i in range(size)])  3.53 us
    all_to_all x1, starting transfers between devices, on_device(): back = lax.all_to_all(made, both, split_axis=0, concat_axis=0, tiled=True)  2.62 us
    pallas_call x1, Pallas kernels, on_device(): call(functools.partial(send_kernel, edge), shape((dp * seq, 2 * cpd, toke...  2.25 us
  transfers between devices with their start and end apart: 4, of which 4 were waited for; matrix products, arithmetic and copies ran while one was open for 0% of the time, Pallas kernels for 19%

profile of v5, /device:TPU:0, one launch (start us, length us, event | category | flops | bytes accessed | tf_op | source)
XLA Modules:
  0.0 49.8 jit_solution(9293723369209406119)
XLA Ops:
  0.6 0.0 copy-start.1
  0.6 2.3 %shard_map.67 = bf16[32,32,256]{2,1,0:T(8,128)(2,1)} custom-call(bf16[256,512]{1,0:T(8,128)(2,1)} %bitcast.9, bf16[256,512]{1,0:T(8,128)(2,1)} %bitcast.12, bf16[256,512]{1,0:T(8,128)(2,1)} %bitcast.13), custom_call_target="tpu_custom_call" | custom-call | bytes 1048576 | tf_op jit(solution)/shard_map/pallas_call | solution.py:377
  2.9 7.3 %all-to-all-start = ((bf16[32,32,256]{2,1,0:T(8,128)(2,1)}), bf16[32,32,256]{2,1,0:T(8,128)(2,1)S(1)}, u32[]{:S(2)}, u32[]{:S(2)}) async-start(bf16[32,32,256]{2,1,0:T(8,128)(2,1)} %shard_map.67), calls=%async_computation | async-start | bytes 1048576 | tf_op jit(solution)/shard_map/all_to_all | solution.py:391
  10.3 0.0 copy-done.1
  10.4 1.8 %collective-permute-start = (f32[1,16,16,128]{3,2,1,0:T(8,128)S(1)}, f32[1,16,16,128]{3,2,1,0:T(8,128)S(1)}, u32[]{:S(2)}, u32[]{:S(2)}) collective-permute-start(f32[1,16,16,128]{3,2,1,0:T(8,128)S(1)} %get-tuple-element.9), channel_id=1, source_target_pairs={{0,16},{16,0},{1,17},{17,1},{2,18},{18,2},{3,19},{19,3},{4,20},{20... | collective-permute-start | bytes 393224 | tf_op jit(solution)/shard_map/ppermute | solution.py:341
  12.2 7.6 %collective-permute-done = f32[1,16,16,128]{3,2,1,0:T(8,128)S(1)} collective-permute-done((f32[1,16,16,128]{3,2,1,0:T(8,128)S(1)}, f32[1,16,16,128]{3,2,1,0:T(8,128)S(1)}, u32[]{:S(2)}, u32[]{:S(2)}) %collective-permute-start) | collective-permute-done | bytes 131104 | tf_op jit(solution)/shard_map/ppermute | solution.py:341
  19.8 0.8 %shard_map.68.ready = bf16[4,2,1024,128]{3,2,1,0:T(8,128)(2,1)S(1)} custom-call(f32[2,16,16,128]{3,2,1,0:T(8,128)S(1)} %constant_dynamic-update-slice_fusion.1.taps), custom_call_target="tpu_custom_call" | custom-call | flops 1073741824 | bytes 1048576 | tf_op jit(solution)/shard_map/pallas_call | solution.py:394
  20.7 5.4 %all-to-all-done.got = bf16[32,32,256]{2,1,0:T(8,128)(2,1)S(1)} async-done(((bf16[32,32,256]{2,1,0:T(8,128)(2,1)}), bf16[32,32,256]{2,1,0:T(8,128)(2,1)S(1)}, u32[]{:S(2)}, u32[]{:S(2)}) %all-to-all-start) | async-done | bytes 524320 | tf_op jit(solution)/shard_map/all_to_all | solution.py:391
  26.1 4.1 %shard_map.69 = bf16[32,32,256]{2,1,0:T(8,128)(2,1)} custom-call(bf16[32,32,256]{2,1,0:T(8,128)(2,1)S(1)} %all-to-all-done.got, f32[2,16,16,128]{3,2,1,0:T(8,128)S(1)} %constant_dynamic-update-slice_fusion.1.taps, bf16[4,2,1024,128]{3,2,1,0:T(8,128)(2,1)S(1)} %shard_map.68.ready), custom_call_target="tpu_custom_call" | custom-call | bytes 1048576 | tf_op jit(solution)/shard_map/pallas_call | solution.py:401
  30.2 2.6 %all-to-all-start.1 = ((bf16[32,32,256]{2,1,0:T(8,128)(2,1)}), bf16[32,32,256]{2,1,0:T(8,128)(2,1)S(1)}, u32[]{:S(2)}, u32[]{:S(2)}) async-start(bf16[32,32,256]{2,1,0:T(8,128)(2,1)} %shard_map.69), calls=%async_computation.1 | async-start | bytes 1048576 | tf_op jit(solution)/shard_map/all_to_all | solution.py:417
  32.9 0.0 copy-start
  32.9 8.8 %shard_map.71 = f32[2,16,2048]{2,1,0:T(8,128)S(1)} custom-call(bf16[32,32,256]{2,1,0:T(8,128)(2,1)S(1)} %all-to-all-done.got), custom_call_target="tpu_custom_call" | custom-call | flops 1073741824 | bytes 1048576 | tf_op jit(solution)/shard_map/pallas_call | solution.py:418
  41.7 1.7 %collective-permute-start.1 = (f32[1,16,2048]{2,1,0:T(8,128)S(1)}, f32[1,16,2048]{2,1,0:T(8,128)S(1)}, u32[]{:S(2)}, u32[]{:S(2)}) collective-permute-start(f32[1,16,2048]{2,1,0:T(8,128)S(1)} %get-tuple-element.7), channel_id=1, source_target_pairs={{0,16},{16,0},{1,17},{17,1},{2,18},{18,2},{3,19},{19,3},{4,20},{20... | collective-permute-start | bytes 393224 | tf_op jit(solution)/shard_map/ppermute | solution.py:341
  43.4 4.8 %collective-permute-done.1 = f32[1,16,2048]{2,1,0:T(8,128)S(1)} collective-permute-done((f32[1,16,2048]{2,1,0:T(8,128)S(1)}, f32[1,16,2048]{2,1,0:T(8,128)S(1)}, u32[]{:S(2)}, u32[]{:S(2)}) %collective-permute-start.1) | collective-permute-done | bytes 131104 | tf_op jit(solution)/shard_map/ppermute | solution.py:341
  48.2 0.0 copy-start.2
  48.2 0.5 %all-to-all-done.1.got = bf16[32,32,256]{2,1,0:T(8,128)(2,1)S(1)} async-done(((bf16[32,32,256]{2,1,0:T(8,128)(2,1)}), bf16[32,32,256]{2,1,0:T(8,128)(2,1)S(1)}, u32[]{:S(2)}, u32[]{:S(2)}) %all-to-all-start.1) | async-done | bytes 524320 | tf_op jit(solution)/shard_map/all_to_all | solution.py:417
  48.7 0.0 copy-done
  48.7 1.1 %shard_map.70 = (bf16[256,512]{1,0:T(8,128)(2,1)}, bf16[256,512]{1,0:T(8,128)(2,1)}) custom-call(bf16[32,32,256]{2,1,0:T(8,128)(2,1)S(1)} %all-to-all-done.1.got, bf16[256,512]{1,0:T(8,128)(2,1)S(1)} %bitcast.10), custom_call_target="tpu_custom_call" | custom-call | bytes 1048576 | tf_op jit(solution)/shard_map/pallas_call | solution.py:434
  49.8 0.0 copy-done.2
  (7 shorter events, 0.2 us)
Async XLA Ops:
  0.6 9.6 %copy-start.1 = (f32[2,16,2048]{2,1,0:T(8,128)S(1)}, f32[2,16,2048]{2,1,0:T(8,128)}, u32[]{:S(2)}) copy-start(f32[2,16,2048]{2,1,0:T(8,128)} %param.7) | copy-start | bytes 786436
  2.9 23.2 %all-to-all-start = ((bf16[32,32,256]{2,1,0:T(8,128)(2,1)}), bf16[32,32,256]{2,1,0:T(8,128)(2,1)S(1)}, u32[]{:S(2)}, u32[]{:S(2)}) async-start(bf16[32,32,256]{2,1,0:T(8,128)(2,1)} %shard_map.67), calls=%async_computation | async-start | bytes 1048576 | tf_op jit(solution)/shard_map/all_to_all | solution.py:391
  10.4 9.4 %collective-permute-start = (f32[1,16,16,128]{3,2,1,0:T(8,128)S(1)}, f32[1,16,16,128]{3,2,1,0:T(8,128)S(1)}, u32[]{:S(2)}, u32[]{:S(2)}) collective-permute-start(f32[1,16,16,128]{3,2,1,0:T(8,128)S(1)} %get-tuple-element.9), channel_id=1, source_target_pairs={{0,16},{16,0},{1,17},{17,1},{2,18},{18,2},{3,19},{19,3},{4,20},{20... | collective-permute-start | bytes 393224 | tf_op jit(solution)/shard_map/ppermute | solution.py:341
  30.2 18.5 %all-to-all-start.1 = ((bf16[32,32,256]{2,1,0:T(8,128)(2,1)}), bf16[32,32,256]{2,1,0:T(8,128)(2,1)S(1)}, u32[]{:S(2)}, u32[]{:S(2)}) async-start(bf16[32,32,256]{2,1,0:T(8,128)(2,1)} %shard_map.69), calls=%async_computation.1 | async-start | bytes 1048576 | tf_op jit(solution)/shard_map/all_to_all | solution.py:417
  32.9 15.9 %copy-start = (bf16[1,256,512]{2,1,0:T(8,128)(2,1)S(1)}, bf16[1,256,512]{2,1,0:T(8,128)(2,1)}, u32[]{:S(2)}) copy-start(bf16[1,256,512]{2,1,0:T(8,128)(2,1)} %param.4) | copy-start | bytes 786436
  41.7 6.5 %collective-permute-start.1 = (f32[1,16,2048]{2,1,0:T(8,128)S(1)}, f32[1,16,2048]{2,1,0:T(8,128)S(1)}, u32[]{:S(2)}, u32[]{:S(2)}) collective-permute-start(f32[1,16,2048]{2,1,0:T(8,128)S(1)} %get-tuple-element.7), channel_id=1, source_target_pairs={{0,16},{16,0},{1,17},{17,1},{2,18},{18,2},{3,19},{19,3},{4,20},{20... | collective-permute-start | bytes 393224 | tf_op jit(solution)/shard_map/ppermute | solution.py:341
  48.2 1.6 %copy-start.2 = (f32[2,16,2048]{2,1,0:T(8,128)}, f32[2,16,2048]{2,1,0:T(8,128)S(1)}, u32[]{:S(2)}) copy-start(f32[2,16,2048]{2,1,0:T(8,128)S(1)} %constant_dynamic-update-slice_fusion) | copy-start | bytes 786436

commit v6 on v5

--- a/solution.py
+++ b/solution.py
@@ -46,14 +46,15 @@
     for copy in coming:
         copy.start()
     flip = flip_matrix(grads.shape[0], bf16)
+    coming[0].wait()
+    turned = [signals[:, pl.ds(p * width, width)].astype(f32).T for p in range(dp)]
+    for copy in coming[1:]:
+        copy.wait()
     for p in range(dp):
         at = pl.ds(p * width, width)
-        if p == 0:
-            for copy in coming:
-                copy.wait()
         scaled = (grads[:, at].astype(f32) * gates[:, at].astype(f32)).T
         scaled = times(scaled.astype(bf16), flip)
-        plain = signals[:, at].astype(f32).T
+        plain = turned[p]
         for q in range(seq):
             parts = []
             for value in (scaled, plain):
@@ -165,7 +166,7 @@
             stream = kind * dp + b
             here = held[kind][half, pl.ds(slots(b, seq, pitch) + c, seq, stride=pitch), :]
             behind = held[kind][half, pl.ds(slots(b, seq, pitch, 0) + c, seq, stride=pitch), :]
-            crossed = pltpu.roll(jnp.where(low, behind, here), small, 1)
+            crossed = pltpu.roll(jnp.where(low, behind, here).astype(bf16), small, 1).astype(f32)
             to = 2 * half * streams + stream
             line[u, pl.ds(to, seq, stride=group + 1), :] = jnp.where(low, here, crossed)
             line[u, pl.ds(to + streams, seq, stride=group + 1), :] = jnp.where(low, crossed, behind)

time: 50.1 us -> 50.1 us (level)
  no operation moved by 1% of the time
where the time goes in v6:
time: 50.1 us; the launch traced here: 49.7 us
  waiting for transfers between devices  18.3 us (37%)
  Pallas kernels  16.9 us (34%)
  starting transfers between devices  13.5 us (27%)
  between operations  0.78 us (2%)
    ppermute x2, waiting for transfers between devices, exchange(): part = lax.ppermute(part, axis, [(i, (i + k) % size) for i in range(size)])  12.4 us
    pallas_call x1, Pallas kernels, on_device(): call(functools.partial(tap_kernel, inner, float(dp * length) ** (-0.5)),...  8.74 us
    all_to_all x1, starting transfers between devices, on_device(): got = lax.all_to_all(sent, both, split_axis=0, concat_axis=0, tiled=True)  7.33 us
    all_to_all x1, waiting for transfers between devices, on_device(): got = lax.all_to_all(sent, both, split_axis=0, concat_axis=0, tiled=True)  5.42 us
    pallas_call x1, Pallas kernels, on_device(): call(functools.partial(mix_kernel, inner), shape((dp * seq, 2 * cpd, toke...  4.02 us
    ppermute x2, starting transfers between devices, exchange(): part = lax.ppermute(part, axis, [(i, (i + k) % size) for i in range(size)])  3.54 us
    all_to_all x1, starting transfers between devices, on_device(): back = lax.all_to_all(made, both, split_axis=0, concat_axis=0, tiled=True)  2.62 us
    pallas_call x1, Pallas kernels, on_device(): call(functools.partial(send_kernel, edge), shape((dp * seq, 2 * cpd, toke...  2.28 us
  transfers between devices with their start and end apart: 4, of which 4 were waited for; matrix products, arithmetic and copies ran while one was open for 0% of the time, Pallas kernels for 19%

profile of v6, /device:TPU:0, one launch (start us, length us, event | category | flops | bytes accessed | tf_op | source)
XLA Modules:
  0.0 49.7 jit_solution(6617533843931661695)
XLA Ops:
  0.6 0.0 copy-start.1
  0.6 2.3 %shard_map.67 = bf16[32,32,256]{2,1,0:T(8,128)(2,1)} custom-call(bf16[256,512]{1,0:T(8,128)(2,1)} %bitcast.9, bf16[256,512]{1,0:T(8,128)(2,1)} %bitcast.12, bf16[256,512]{1,0:T(8,128)(2,1)} %bitcast.13), custom_call_target="tpu_custom_call" | custom-call | bytes 1048576 | tf_op jit(solution)/shard_map/pallas_call | solution.py:378
  2.9 7.3 %all-to-all-start = ((bf16[32,32,256]{2,1,0:T(8,128)(2,1)}), bf16[32,32,256]{2,1,0:T(8,128)(2,1)S(1)}, u32[]{:S(2)}, u32[]{:S(2)}) async-start(bf16[32,32,256]{2,1,0:T(8,128)(2,1)} %shard_map.67), calls=%async_computation | async-start | bytes 1048576 | tf_op jit(solution)/shard_map/all_to_all | solution.py:392
  10.3 0.0 copy-done.1
  10.4 1.8 %collective-permute-start = (f32[1,16,16,128]{3,2,1,0:T(8,128)S(1)}, f32[1,16,16,128]{3,2,1,0:T(8,128)S(1)}, u32[]{:S(2)}, u32[]{:S(2)}) collective-permute-start(f32[1,16,16,128]{3,2,1,0:T(8,128)S(1)} %get-tuple-element.9), channel_id=1, source_target_pairs={{0,16},{16,0},{1,17},{17,1},{2,18},{18,2},{3,19},{19,3},{4,20},{20... | collective-permute-start | bytes 393224 | tf_op jit(solution)/shard_map/ppermute | solution.py:342
  12.3 7.6 %collective-permute-done = f32[1,16,16,128]{3,2,1,0:T(8,128)S(1)} collective-permute-done((f32[1,16,16,128]{3,2,1,0:T(8,128)S(1)}, f32[1,16,16,128]{3,2,1,0:T(8,128)S(1)}, u32[]{:S(2)}, u32[]{:S(2)}) %collective-permute-start) | collective-permute-done | bytes 131104 | tf_op jit(solution)/shard_map/ppermute | solution.py:342
  19.9 0.8 %shard_map.68.ready = bf16[4,2,1024,128]{3,2,1,0:T(8,128)(2,1)S(1)} custom-call(f32[2,16,16,128]{3,2,1,0:T(8,128)S(1)} %constant_dynamic-update-slice_fusion.1.taps), custom_call_target="tpu_custom_call" | custom-call | flops 1073741824 | bytes 1048576 | tf_op jit(solution)/shard_map/pallas_call | solution.py:395
  20.7 5.4 %all-to-all-done.got = bf16[32,32,256]{2,1,0:T(8,128)(2,1)S(1)} async-done(((bf16[32,32,256]{2,1,0:T(8,128)(2,1)}), bf16[32,32,256]{2,1,0:T(8,128)(2,1)S(1)}, u32[]{:S(2)}, u32[]{:S(2)}) %all-to-all-start) | async-done | bytes 524320 | tf_op jit(solution)/shard_map/all_to_all | solution.py:392
  26.1 4.0 %shard_map.69 = bf16[32,32,256]{2,1,0:T(8,128)(2,1)} custom-call(bf16[32,32,256]{2,1,0:T(8,128)(2,1)S(1)} %all-to-all-done.got, f32[2,16,16,128]{3,2,1,0:T(8,128)S(1)} %constant_dynamic-update-slice_fusion.1.taps, bf16[4,2,1024,128]{3,2,1,0:T(8,128)(2,1)S(1)} %shard_map.68.ready), custom_call_target="tpu_custom_call" | custom-call | bytes 1048576 | tf_op jit(solution)/shard_map/pallas_call | solution.py:402
  30.2 2.6 %all-to-all-start.1 = ((bf16[32,32,256]{2,1,0:T(8,128)(2,1)}), bf16[32,32,256]{2,1,0:T(8,128)(2,1)S(1)}, u32[]{:S(2)}, u32[]{:S(2)}) async-start(bf16[32,32,256]{2,1,0:T(8,128)(2,1)} %shard_map.69), calls=%async_computation.1 | async-start | bytes 1048576 | tf_op jit(solution)/shard_map/all_to_all | solution.py:418
  32.8 0.0 copy-start
  32.8 8.7 %shard_map.71 = f32[2,16,2048]{2,1,0:T(8,128)S(1)} custom-call(bf16[32,32,256]{2,1,0:T(8,128)(2,1)S(1)} %all-to-all-done.got), custom_call_target="tpu_custom_call" | custom-call | flops 1073741824 | bytes 1048576 | tf_op jit(solution)/shard_map/pallas_call | solution.py:419
  41.6 1.7 %collective-permute-start.1 = (f32[1,16,2048]{2,1,0:T(8,128)S(1)}, f32[1,16,2048]{2,1,0:T(8,128)S(1)}, u32[]{:S(2)}, u32[]{:S(2)}) collective-permute-start(f32[1,16,2048]{2,1,0:T(8,128)S(1)} %get-tuple-element.7), channel_id=1, source_target_pairs={{0,16},{16,0},{1,17},{17,1},{2,18},{18,2},{3,19},{19,3},{4,20},{20... | collective-permute-start | bytes 393224 | tf_op jit(solution)/shard_map/ppermute | solution.py:342
  43.3 4.8 %collective-permute-done.1 = f32[1,16,2048]{2,1,0:T(8,128)S(1)} collective-permute-done((f32[1,16,2048]{2,1,0:T(8,128)S(1)}, f32[1,16,2048]{2,1,0:T(8,128)S(1)}, u32[]{:S(2)}, u32[]{:S(2)}) %collective-permute-start.1) | collective-permute-done | bytes 131104 | tf_op jit(solution)/shard_map/ppermute | solution.py:342
  48.2 0.0 copy-start.2
  48.2 0.5 %all-to-all-done.1.got = bf16[32,32,256]{2,1,0:T(8,128)(2,1)S(1)} async-done(((bf16[32,32,256]{2,1,0:T(8,128)(2,1)}), bf16[32,32,256]{2,1,0:T(8,128)(2,1)S(1)}, u32[]{:S(2)}, u32[]{:S(2)}) %all-to-all-start.1) | async-done | bytes 524320 | tf_op jit(solution)/shard_map/all_to_all | solution.py:418
  48.7 0.0 copy-done
  48.7 1.1 %shard_map.70 = (bf16[256,512]{1,0:T(8,128)(2,1)}, bf16[256,512]{1,0:T(8,128)(2,1)}) custom-call(bf16[32,32,256]{2,1,0:T(8,128)(2,1)S(1)} %all-to-all-done.1.got, bf16[256,512]{1,0:T(8,128)(2,1)S(1)} %bitcast.10), custom_call_target="tpu_custom_call" | custom-call | bytes 1048576 | tf_op jit(solution)/shard_map/pallas_call | solution.py:435
  49.7 0.0 copy-done.2
  (7 shorter events, 0.2 us)
Async XLA Ops:
  0.6 9.7 %copy-start.1 = (f32[2,16,2048]{2,1,0:T(8,128)S(1)}, f32[2,16,2048]{2,1,0:T(8,128)}, u32[]{:S(2)}) copy-start(f32[2,16,2048]{2,1,0:T(8,128)} %param.7) | copy-start | bytes 786436
  2.9 23.2 %all-to-all-start = ((bf16[32,32,256]{2,1,0:T(8,128)(2,1)}), bf16[32,32,256]{2,1,0:T(8,128)(2,1)S(1)}, u32[]{:S(2)}, u32[]{:S(2)}) async-start(bf16[32,32,256]{2,1,0:T(8,128)(2,1)} %shard_map.67), calls=%async_computation | async-start | bytes 1048576 | tf_op jit(solution)/shard_map/all_to_all | solution.py:392
  10.4 9.4 %collective-permute-start = (f32[1,16,16,128]{3,2,1,0:T(8,128)S(1)}, f32[1,16,16,128]{3,2,1,0:T(8,128)S(1)}, u32[]{:S(2)}, u32[]{:S(2)}) collective-permute-start(f32[1,16,16,128]{3,2,1,0:T(8,128)S(1)} %get-tuple-element.9), channel_id=1, source_target_pairs={{0,16},{16,0},{1,17},{17,1},{2,18},{18,2},{3,19},{19,3},{4,20},{20... | collective-permute-start | bytes 393224 | tf_op jit(solution)/shard_map/ppermute | solution.py:342
  30.2 18.5 %all-to-all-start.1 = ((bf16[32,32,256]{2,1,0:T(8,128)(2,1)}), bf16[32,32,256]{2,1,0:T(8,128)(2,1)S(1)}, u32[]{:S(2)}, u32[]{:S(2)}) async-start(bf16[32,32,256]{2,1,0:T(8,128)(2,1)} %shard_map.69), calls=%async_computation.1 | async-start | bytes 1048576 | tf_op jit(solution)/shard_map/all_to_all | solution.py:418
  32.8 15.9 %copy-start = (bf16[1,256,512]{2,1,0:T(8,128)(2,1)S(1)}, bf16[1,256,512]{2,1,0:T(8,128)(2,1)}, u32[]{:S(2)}) copy-start(bf16[1,256,512]{2,1,0:T(8,128)(2,1)} %param.4) | copy-start | bytes 786436
  41.6 6.5 %collective-permute-start.1 = (f32[1,16,2048]{2,1,0:T(8,128)S(1)}, f32[1,16,2048]{2,1,0:T(8,128)S(1)}, u32[]{:S(2)}, u32[]{:S(2)}) collective-permute-start(f32[1,16,2048]{2,1,0:T(8,128)S(1)} %get-tuple-element.7), channel_id=1, source_target_pairs={{0,16},{16,0},{1,17},{17,1},{2,18},{18,2},{3,19},{19,3},{4,20},{20... | collective-permute-start | bytes 393224 | tf_op jit(solution)/shard_map/ppermute | solution.py:342
  48.2 1.6 %copy-start.2 = (f32[2,16,2048]{2,1,0:T(8,128)}, f32[2,16,2048]{2,1,0:T(8,128)S(1)}, u32[]{:S(2)}) copy-start(f32[2,16,2048]{2,1,0:T(8,128)S(1)} %constant_dynamic-update-slice_fusion) | copy-start | bytes 786436
